TPU v7x, 128 devices: a whole 4x4x4 slice. The times are simulated.
128 devices in a mesh: batch: 1, cols: 16 (over z, y), rows: 8 (over x, core).
Axes of the slice: x: 4, y: 4, z: 4, core: 2. Of those that a mesh axis runs over, the one named last changes fastest.
Arguments:
- frames: bfloat16 [8, 2, 128, 256, 192], P(None, 'batch', 'rows', 'cols')
- w_x: bfloat16 [3, 3, 192, 768], replicated
- w_h: bfloat16 [3, 3, 192, 768], replicated
- gate_bias: float32 [768], replicated
- h_init: bfloat16 [2, 128, 256, 192], P('batch', 'rows', 'cols')
- c_init: float32 [2, 128, 256, 192], P('batch', 'rows', 'cols')
Outputs:
- output 1: bfloat16 [8, 2, 128, 256, 192], P(None, 'batch', 'rows', 'cols')
- output 2: float32 [2, 128, 256, 192], P('batch', 'rows', 'cols')
All inputs are finite; a program needn't handle non-finite values.
Results may differ from a plain program's by a relative error of at most 0.00162075.
Values are sent between devices in bfloat16 or wider.
A program may use at most 1 GiB of HBM per device.

v0:
```python
import jax
import jax.numpy as jnp
from jax import lax
from jax.sharding import PartitionSpec as P, NamedSharding


def edge_swap(tile_arr, halo_width, split_dim, axis_label, axis_count):
    length = tile_arr.shape[split_dim]
    low_edge = lax.slice_in_dim(tile_arr, 0, halo_width, axis=split_dim)
    high_edge = lax.slice_in_dim(tile_arr, length - halo_width, length, axis=split_dim)
    down_pairs = [(source, source + 1) for source in range(axis_count - 1)]
    up_pairs = [(source + 1, source) for source in range(axis_count - 1)]
    from_prev = lax.ppermute(high_edge, axis_label, down_pairs)
    from_next = lax.ppermute(low_edge, axis_label, up_pairs)
    return jnp.concatenate([from_prev, tile_arr, from_next], axis=split_dim)


def with_halo(tile_arr, halo_width, row_dim, row_count, col_count):
    row_ext = edge_swap(tile_arr, halo_width, row_dim, "rows", row_count)
    return edge_swap(row_ext, halo_width, row_dim + 1, "cols", col_count)


def conv_taps(padded, weights, out_rows, out_cols):
    tap_list = [padded[:, row_off:row_off + out_rows, col_off:col_off + out_cols, :] for row_off in range(3) for col_off in range(3)]
    patches = jnp.concatenate(tap_list, axis=-1)
    flat_patches = patches.reshape(-1, patches.shape[-1])
    flat_weights = weights.reshape(-1, weights.shape[-1])
    product = jnp.dot(flat_patches, flat_weights, preferred_element_type=jnp.float32)
    return product.reshape(padded.shape[0], out_rows, out_cols, -1)


def lstm_cell(gate_sum, cell_prev):
    hidden_width = cell_prev.shape[-1]
    in_gate = jax.nn.sigmoid(gate_sum[..., :hidden_width])
    forget_gate = jax.nn.sigmoid(gate_sum[..., hidden_width:2 * hidden_width])
    out_gate = jax.nn.sigmoid(gate_sum[..., 2 * hidden_width:3 * hidden_width])
    cand_gate = jnp.tanh(gate_sum[..., 3 * hidden_width:])
    cell_next = forget_gate * cell_prev + in_gate * cand_gate
    hidden_next = (out_gate * jnp.tanh(cell_next)).astype(jnp.bfloat16)
    return hidden_next, cell_next


def solution(mesh):
    row_count = mesh.shape["rows"]
    col_count = mesh.shape["cols"]
    frame_spec = P(None, "batch", "rows", "cols", None)
    state_spec = P("batch", "rows", "cols", None)

    def local_run(frames, w_x, w_h, gate_bias, h_init, c_init):
        tile_rows = h_init.shape[1]
        tile_cols = h_init.shape[2]
        frames_ext = with_halo(frames, 1, 2, row_count, col_count)

        def step_fn(state_pair, frame_ext):
            hidden, cell_state = state_pair
            hidden_ext = with_halo(hidden, 1, 1, row_count, col_count)
            gate_sum = conv_taps(frame_ext, w_x, tile_rows, tile_cols) + conv_taps(hidden_ext, w_h, tile_rows, tile_cols) + gate_bias
            hidden_next, cell_next = lstm_cell(gate_sum, cell_state)
            return (hidden_next, cell_next), hidden_next

        final_pair, all_hidden = lax.scan(step_fn, (h_init, c_init), frames_ext)
        return all_hidden, final_pair[1]

    return jax.shard_map(local_run, mesh=mesh, in_specs=(frame_spec, P(), P(), P(), state_spec, state_spec), out_specs=(frame_spec, state_spec), check_vma=False)
```

profile of v0, /device:TPU:97, one launch (start us, length us, event | category | flops | bytes accessed | tf_op | source)
XLA Modules:
  0.0 315.1 jit_solution(661347327891288076)
XLA Ops:
  3.6 3.7 %collective-permute-start.4 = (bf16[8,2,1,16,192]{4,3,2,1,0:T(8,128)(2,1)S(1)}, bf16[8,2,1,16,192]{4,3,2,1,0:T(8,128)(2,1)S(1)}, u32[]{:S(2)}, u32[]{:S(2)}) collective-permute-start(bf16[8,2,1,16,192]{4,3,2,1,0:T(8,128)(2,1)S(1)} %get-tuple-element.94), channel_id=1, source_target_pairs={{0,1},{1,2},{2,3},{3,4},{4,5},{5,6},{6,7},{8,9},{9,10},{10,11},{11... | collective-permute-start | bytes 294920 | tf_op jit(solution)/shard_map/ppermute | solution.py:13
  9.5 4.1 %collective-permute-done.5 = bf16[8,2,1,16,192]{4,3,2,1,0:T(8,128)(2,1)S(1)} collective-permute-done((bf16[8,2,1,16,192]{4,3,2,1,0:T(8,128)(2,1)S(1)}, bf16[8,2,1,16,192]{4,3,2,1,0:T(8,128)(2,1)S(1)}, u32[]{:S(2)}, u32[]{:S(2)}) %collective-permute-start.5) | collective-permute-done | bytes 98336 | tf_op jit(solution)/shard_map/ppermute | solution.py:14
  15.5 4.5 %collective-permute-start.7 = (bf16[8,2,18,1,192]{4,3,2,1,0:T(2,128)(2,1)S(1)}, bf16[8,2,18,1,192]{4,3,2,1,0:T(2,128)(2,1)S(1)}, u32[]{:S(2)}, u32[]{:S(2)}) collective-permute-start(bf16[8,2,18,1,192]{4,3,2,1,0:T(2,128)(2,1)S(1)} %get-tuple-element.92), channel_id=1, source_target_pairs={{8,0},{16,8},{24,16},{32,24},{40,32},{48,40},{56,48},{64,56},{72,6... | collective-permute-start | bytes 331784 | tf_op jit(solution)/shard_map/ppermute | solution.py:14
  22.0 2.6 collective-permute-done.7
  24.6 6.2 %collective-permute-done.6 = bf16[8,2,18,1,192]{4,3,2,1,0:T(2,128)(2,1)S(1)} collective-permute-done((bf16[8,2,18,1,192]{4,3,2,1,0:T(2,128)(2,1)S(1)}, bf16[8,2,18,1,192]{4,3,2,1,0:T(2,128)(2,1)S(1)}, u32[]{:S(2)}, u32[]{:S(2)}) %collective-permute-start.6) | collective-permute-done | bytes 110624 | tf_op jit(solution)/shard_map/ppermute | solution.py:13
  30.8 4.9 %pad_maximum_fusion.4 = bf16[8,2,18,18,192]{4,3,2,1,0:T(8,128)(2,1)} fusion(bf16[8,2,18,1,192]{4,3,2,1,0:T(2,128)(2,1)S(1)} %collective-permute-done.7, bf16[8,2,18,16,192]{4,3,2,1,0:T(8,128)(2,1)} %copy-done.4, bf16[8,2,18,1,192]{4,3,2,1,0:T(2,128)(2,1)S(1)} %collective-permute-done.6), kind=kLoop, calls=%fused_computation.40 | loop fusion | flops 5971968 | bytes 3981312 | tf_op jit(solution)/shard_map/concatenate | solution.py:15
  35.7 279.4 %while.14 = (s32[]{:T(128)}, bf16[2,16,16,192]{3,2,1,0:T(8,128)(2,1)S(1)}, f32[2,16,16,192]{3,2,1,0:T(8,128)}, bf16[8,2,16,16,192]{4,3,2,1,0:T(8,128)(2,1)}, bf1...) while((s32[]{:T(128)}, ...), condition=%wide.region_1.2_spmd, body=%wide.region_0.1_spmd.sunk | while | flops 2723217408 | bytes 34416992 | solution.py:61
  37.6 4.7 %collective-permute-start.1 = (bf16[2,1,16,192]{3,2,1,0:T(8,128)(2,1)S(1)}, bf16[2,1,16,192]{3,2,1,0:T(8,128)(2,1)S(1)}, u32[]{:S(2)}, u32[]{:S(2)}) collective-permute-start(bf16[2,1,16,192]{3,2,1,0:T(8,128)(2,1)S(1)} %get-tuple-element.179), channel_id=1, source_target_pairs={{0,1},{1,2},{2,3},{3,4},{4,5},{5,6},{6,7},{8,9},{9,10},{10,11},{11... | collective-permute-start | bytes 36872 | tf_op jit(solution)/shard_map/while/body/eval_jaxpr/ppermute | solution.py:13
  49.9 3.4 %collective-permute-start.3 = (bf16[2,18,1,192]{3,2,1,0:T(2,128)(2,1)S(1)}, bf16[2,18,1,192]{3,2,1,0:T(2,128)(2,1)S(1)}, u32[]{:S(2)}, u32[]{:S(2)}) collective-permute-start(bf16[2,18,1,192]{3,2,1,0:T(2,128)(2,1)S(1)} %get-tuple-element.182), channel_id=1, source_target_pairs={{0,8},{8,16},{16,24},{24,32},{32,40},{40,48},{48,56},{56,64},{64,7... | collective-permute-start | bytes 41480 | tf_op jit(solution)/shard_map/while/body/eval_jaxpr/ppermute | solution.py:13
  53.3 4.5 %fusion.43 = f32[2,16,16,768]{3,2,1,0:T(8,128)} fusion(bf16[2,16,16,1728]{3,2,1,0:T(8,128)(2,1)S(1)} %concatenate.36, bf16[1728,768,1,1]{1,0,3,2:T(8,128)(2,1)} %bitcast.34), kind=kOutput, calls=%fused_computation.49.clone.1 | convolution fusion | flops 1358954496 | bytes 5996544 | tf_op jit(solution)/shard_map/while/body/eval_jaxpr/dot_general | solution.py:28
  57.8 3.3 %pad_maximum_fusion.8 = (bf16[2,16,16,192]{3,2,1,0:T(8,128)(2,1)S(1)}, bf16[2,16,16,192]{3,2,1,0:T(8,128)(2,1)S(1)}, bf16[2,16,16,192]{3,2,1,0:T(8,128)(2,1)S(1)...) fusion(bf16[2,18,1,192]{3,2,1,0:T(2,128)(2,1)S(1)} %collective-per, ...), kind=kLoop, calls=%fused_computation.32.clone.1 | loop fusion | flops 2359296 | bytes 1428480 | tf_op jit(solution)/shard_map/while/body/eval_jaxpr/concatenate | solution.py:15
  63.6 3.9 %add_add_fusion.2 = f32[2,16,16,768]{3,2,1,0:T(8,128)S(1)} fusion(f32[2,16,16,768]{3,2,1,0:T(8,128)} %fusion.43, bf16[2,16,16,1728]{3,2,1,0:T(8,128)(2,1)S(1)} %concatenate.37, bf16[1728,768,1,1]{1,0,3,2:T(8,128)(2,1)} %bitcast.35, f32[768]{0:T(1024)S(1)} %get-tuple-element.219), kind=kOutput, calls=%fused_computation.clone.1 | convolution fusion | flops 1359740928 | bytes 7572480 | tf_op jit(solution)/shard_map/while/body/eval_jaxpr/dot_general | solution.py:28
  71.7 3.6 %collective-permute-start.1 = (bf16[2,1,16,192]{3,2,1,0:T(8,128)(2,1)S(1)}, bf16[2,1,16,192]{3,2,1,0:T(8,128)(2,1)S(1)}, u32[]{:S(2)}, u32[]{:S(2)}) collective-permute-start(bf16[2,1,16,192]{3,2,1,0:T(8,128)(2,1)S(1)} %get-tuple-element.179), channel_id=1, source_target_pairs={{0,1},{1,2},{2,3},{3,4},{4,5},{5,6},{6,7},{8,9},{9,10},{10,11},{11... | collective-permute-start | bytes 36872 | tf_op jit(solution)/shard_map/while/body/eval_jaxpr/ppermute | solution.py:13
  81.1 4.0 %collective-permute-start.2 = (bf16[2,18,1,192]{3,2,1,0:T(2,128)(2,1)S(1)}, bf16[2,18,1,192]{3,2,1,0:T(2,128)(2,1)S(1)}, u32[]{:S(2)}, u32[]{:S(2)}) collective-permute-start(bf16[2,18,1,192]{3,2,1,0:T(2,128)(2,1)S(1)} %get-tuple-element.181), channel_id=1, source_target_pairs={{8,0},{16,8},{24,16},{32,24},{40,32},{48,40},{56,48},{64,56},{72,6... | collective-permute-start | bytes 41480 | tf_op jit(solution)/shard_map/while/body/eval_jaxpr/ppermute | solution.py:14
  87.1 4.5 %fusion.43 = f32[2,16,16,768]{3,2,1,0:T(8,128)} fusion(bf16[2,16,16,1728]{3,2,1,0:T(8,128)(2,1)S(1)} %concatenate.36, bf16[1728,768,1,1]{1,0,3,2:T(8,128)(2,1)} %bitcast.34), kind=kOutput, calls=%fused_computation.49.clone.1 | convolution fusion | flops 1358954496 | bytes 5996544 | tf_op jit(solution)/shard_map/while/body/eval_jaxpr/dot_general | solution.py:28
  91.9 3.3 %pad_maximum_fusion.8 = (bf16[2,16,16,192]{3,2,1,0:T(8,128)(2,1)S(1)}, bf16[2,16,16,192]{3,2,1,0:T(8,128)(2,1)S(1)}, bf16[2,16,16,192]{3,2,1,0:T(8,128)(2,1)S(1)...) fusion(bf16[2,18,1,192]{3,2,1,0:T(2,128)(2,1)S(1)} %collective-per, ...), kind=kLoop, calls=%fused_computation.32.clone.1 | loop fusion | flops 2359296 | bytes 1428480 | tf_op jit(solution)/shard_map/while/body/eval_jaxpr/concatenate | solution.py:15
  97.8 3.9 %add_add_fusion.2 = f32[2,16,16,768]{3,2,1,0:T(8,128)S(1)} fusion(f32[2,16,16,768]{3,2,1,0:T(8,128)} %fusion.43, bf16[2,16,16,1728]{3,2,1,0:T(8,128)(2,1)S(1)} %concatenate.37, bf16[1728,768,1,1]{1,0,3,2:T(8,128)(2,1)} %bitcast.35, f32[768]{0:T(1024)S(1)} %get-tuple-element.219), kind=kOutput, calls=%fused_computation.clone.1 | convolution fusion | flops 1359740928 | bytes 7572480 | tf_op jit(solution)/shard_map/while/body/eval_jaxpr/dot_general | solution.py:28
  106.1 3.7 %collective-permute-start.1 = (bf16[2,1,16,192]{3,2,1,0:T(8,128)(2,1)S(1)}, bf16[2,1,16,192]{3,2,1,0:T(8,128)(2,1)S(1)}, u32[]{:S(2)}, u32[]{:S(2)}) collective-permute-start(bf16[2,1,16,192]{3,2,1,0:T(8,128)(2,1)S(1)} %get-tuple-element.179), channel_id=1, source_target_pairs={{0,1},{1,2},{2,3},{3,4},{4,5},{5,6},{6,7},{8,9},{9,10},{10,11},{11... | collective-permute-start | bytes 36872 | tf_op jit(solution)/shard_map/while/body/eval_jaxpr/ppermute | solution.py:13
  112.0 2.6 concatenate.36
  115.5 4.9 %collective-permute-start.2 = (bf16[2,18,1,192]{3,2,1,0:T(2,128)(2,1)S(1)}, bf16[2,18,1,192]{3,2,1,0:T(2,128)(2,1)S(1)}, u32[]{:S(2)}, u32[]{:S(2)}) collective-permute-start(bf16[2,18,1,192]{3,2,1,0:T(2,128)(2,1)S(1)} %get-tuple-element.181), channel_id=1, source_target_pairs={{8,0},{16,8},{24,16},{32,24},{40,32},{48,40},{56,48},{64,56},{72,6... | collective-permute-start | bytes 41480 | tf_op jit(solution)/shard_map/while/body/eval_jaxpr/ppermute | solution.py:14
  122.3 4.5 %fusion.43 = f32[2,16,16,768]{3,2,1,0:T(8,128)} fusion(bf16[2,16,16,1728]{3,2,1,0:T(8,128)(2,1)S(1)} %concatenate.36, bf16[1728,768,1,1]{1,0,3,2:T(8,128)(2,1)} %bitcast.34), kind=kOutput, calls=%fused_computation.49.clone.1 | convolution fusion | flops 1358954496 | bytes 5996544 | tf_op jit(solution)/shard_map/while/body/eval_jaxpr/dot_general | solution.py:28
  127.1 3.3 %pad_maximum_fusion.8 = (bf16[2,16,16,192]{3,2,1,0:T(8,128)(2,1)S(1)}, bf16[2,16,16,192]{3,2,1,0:T(8,128)(2,1)S(1)}, bf16[2,16,16,192]{3,2,1,0:T(8,128)(2,1)S(1)...) fusion(bf16[2,18,1,192]{3,2,1,0:T(2,128)(2,1)S(1)} %collective-per, ...), kind=kLoop, calls=%fused_computation.32.clone.1 | loop fusion | flops 2359296 | bytes 1428480 | tf_op jit(solution)/shard_map/while/body/eval_jaxpr/concatenate | solution.py:15
  133.0 3.9 %add_add_fusion.2 = f32[2,16,16,768]{3,2,1,0:T(8,128)S(1)} fusion(f32[2,16,16,768]{3,2,1,0:T(8,128)} %fusion.43, bf16[2,16,16,1728]{3,2,1,0:T(8,128)(2,1)S(1)} %concatenate.37, bf16[1728,768,1,1]{1,0,3,2:T(8,128)(2,1)} %bitcast.35, f32[768]{0:T(1024)S(1)} %get-tuple-element.219), kind=kOutput, calls=%fused_computation.clone.1 | convolution fusion | flops 1359740928 | bytes 7572480 | tf_op jit(solution)/shard_map/while/body/eval_jaxpr/dot_general | solution.py:28
  141.2 3.7 %collective-permute-start.1 = (bf16[2,1,16,192]{3,2,1,0:T(8,128)(2,1)S(1)}, bf16[2,1,16,192]{3,2,1,0:T(8,128)(2,1)S(1)}, u32[]{:S(2)}, u32[]{:S(2)}) collective-permute-start(bf16[2,1,16,192]{3,2,1,0:T(8,128)(2,1)S(1)} %get-tuple-element.179), channel_id=1, source_target_pairs={{0,1},{1,2},{2,3},{3,4},{4,5},{5,6},{6,7},{8,9},{9,10},{10,11},{11... | collective-permute-start | bytes 36872 | tf_op jit(solution)/shard_map/while/body/eval_jaxpr/ppermute | solution.py:13
  150.7 4.9 %collective-permute-start.2 = (bf16[2,18,1,192]{3,2,1,0:T(2,128)(2,1)S(1)}, bf16[2,18,1,192]{3,2,1,0:T(2,128)(2,1)S(1)}, u32[]{:S(2)}, u32[]{:S(2)}) collective-permute-start(bf16[2,18,1,192]{3,2,1,0:T(2,128)(2,1)S(1)} %get-tuple-element.181), channel_id=1, source_target_pairs={{8,0},{16,8},{24,16},{32,24},{40,32},{48,40},{56,48},{64,56},{72,6... | collective-permute-start | bytes 41480 | tf_op jit(solution)/shard_map/while/body/eval_jaxpr/ppermute | solution.py:14
  157.4 4.5 %fusion.43 = f32[2,16,16,768]{3,2,1,0:T(8,128)} fusion(bf16[2,16,16,1728]{3,2,1,0:T(8,128)(2,1)S(1)} %concatenate.36, bf16[1728,768,1,1]{1,0,3,2:T(8,128)(2,1)} %bitcast.34), kind=kOutput, calls=%fused_computation.49.clone.1 | convolution fusion | flops 1358954496 | bytes 5996544 | tf_op jit(solution)/shard_map/while/body/eval_jaxpr/dot_general | solution.py:28
  162.3 3.3 %pad_maximum_fusion.8 = (bf16[2,16,16,192]{3,2,1,0:T(8,128)(2,1)S(1)}, bf16[2,16,16,192]{3,2,1,0:T(8,128)(2,1)S(1)}, bf16[2,16,16,192]{3,2,1,0:T(8,128)(2,1)S(1)...) fusion(bf16[2,18,1,192]{3,2,1,0:T(2,128)(2,1)S(1)} %collective-per, ...), kind=kLoop, calls=%fused_computation.32.clone.1 | loop fusion | flops 2359296 | bytes 1428480 | tf_op jit(solution)/shard_map/while/body/eval_jaxpr/concatenate | solution.py:15
  168.2 3.9 %add_add_fusion.2 = f32[2,16,16,768]{3,2,1,0:T(8,128)S(1)} fusion(f32[2,16,16,768]{3,2,1,0:T(8,128)} %fusion.43, bf16[2,16,16,1728]{3,2,1,0:T(8,128)(2,1)S(1)} %concatenate.37, bf16[1728,768,1,1]{1,0,3,2:T(8,128)(2,1)} %bitcast.35, f32[768]{0:T(1024)S(1)} %get-tuple-element.219), kind=kOutput, calls=%fused_computation.clone.1 | convolution fusion | flops 1359740928 | bytes 7572480 | tf_op jit(solution)/shard_map/while/body/eval_jaxpr/dot_general | solution.py:28
  176.4 3.7 %collective-permute-start.1 = (bf16[2,1,16,192]{3,2,1,0:T(8,128)(2,1)S(1)}, bf16[2,1,16,192]{3,2,1,0:T(8,128)(2,1)S(1)}, u32[]{:S(2)}, u32[]{:S(2)}) collective-permute-start(bf16[2,1,16,192]{3,2,1,0:T(8,128)(2,1)S(1)} %get-tuple-element.179), channel_id=1, source_target_pairs={{0,1},{1,2},{2,3},{3,4},{4,5},{5,6},{6,7},{8,9},{9,10},{10,11},{11... | collective-permute-start | bytes 36872 | tf_op jit(solution)/shard_map/while/body/eval_jaxpr/ppermute | solution.py:13
  185.9 4.9 %collective-permute-start.2 = (bf16[2,18,1,192]{3,2,1,0:T(2,128)(2,1)S(1)}, bf16[2,18,1,192]{3,2,1,0:T(2,128)(2,1)S(1)}, u32[]{:S(2)}, u32[]{:S(2)}) collective-permute-start(bf16[2,18,1,192]{3,2,1,0:T(2,128)(2,1)S(1)} %get-tuple-element.181), channel_id=1, source_target_pairs={{8,0},{16,8},{24,16},{32,24},{40,32},{48,40},{56,48},{64,56},{72,6... | collective-permute-start | bytes 41480 | tf_op jit(solution)/shard_map/while/body/eval_jaxpr/ppermute | solution.py:14
  192.6 4.5 %fusion.43 = f32[2,16,16,768]{3,2,1,0:T(8,128)} fusion(bf16[2,16,16,1728]{3,2,1,0:T(8,128)(2,1)S(1)} %concatenate.36, bf16[1728,768,1,1]{1,0,3,2:T(8,128)(2,1)} %bitcast.34), kind=kOutput, calls=%fused_computation.49.clone.1 | convolution fusion | flops 1358954496 | bytes 5996544 | tf_op jit(solution)/shard_map/while/body/eval_jaxpr/dot_general | solution.py:28
  197.5 3.3 %pad_maximum_fusion.8 = (bf16[2,16,16,192]{3,2,1,0:T(8,128)(2,1)S(1)}, bf16[2,16,16,192]{3,2,1,0:T(8,128)(2,1)S(1)}, bf16[2,16,16,192]{3,2,1,0:T(8,128)(2,1)S(1)...) fusion(bf16[2,18,1,192]{3,2,1,0:T(2,128)(2,1)S(1)} %collective-per, ...), kind=kLoop, calls=%fused_computation.32.clone.1 | loop fusion | flops 2359296 | bytes 1428480 | tf_op jit(solution)/shard_map/while/body/eval_jaxpr/concatenate | solution.py:15
  203.3 3.9 %add_add_fusion.2 = f32[2,16,16,768]{3,2,1,0:T(8,128)S(1)} fusion(f32[2,16,16,768]{3,2,1,0:T(8,128)} %fusion.43, bf16[2,16,16,1728]{3,2,1,0:T(8,128)(2,1)S(1)} %concatenate.37, bf16[1728,768,1,1]{1,0,3,2:T(8,128)(2,1)} %bitcast.35, f32[768]{0:T(1024)S(1)} %get-tuple-element.219), kind=kOutput, calls=%fused_computation.clone.1 | convolution fusion | flops 1359740928 | bytes 7572480 | tf_op jit(solution)/shard_map/while/body/eval_jaxpr/dot_general | solution.py:28
  211.6 3.7 %collective-permute-start.1 = (bf16[2,1,16,192]{3,2,1,0:T(8,128)(2,1)S(1)}, bf16[2,1,16,192]{3,2,1,0:T(8,128)(2,1)S(1)}, u32[]{:S(2)}, u32[]{:S(2)}) collective-permute-start(bf16[2,1,16,192]{3,2,1,0:T(8,128)(2,1)S(1)} %get-tuple-element.179), channel_id=1, source_target_pairs={{0,1},{1,2},{2,3},{3,4},{4,5},{5,6},{6,7},{8,9},{9,10},{10,11},{11... | collective-permute-start | bytes 36872 | tf_op jit(solution)/shard_map/while/body/eval_jaxpr/ppermute | solution.py:13
  221.0 4.9 %collective-permute-start.2 = (bf16[2,18,1,192]{3,2,1,0:T(2,128)(2,1)S(1)}, bf16[2,18,1,192]{3,2,1,0:T(2,128)(2,1)S(1)}, u32[]{:S(2)}, u32[]{:S(2)}) collective-permute-start(bf16[2,18,1,192]{3,2,1,0:T(2,128)(2,1)S(1)} %get-tuple-element.181), channel_id=1, source_target_pairs={{8,0},{16,8},{24,16},{32,24},{40,32},{48,40},{56,48},{64,56},{72,6... | collective-permute-start | bytes 41480 | tf_op jit(solution)/shard_map/while/body/eval_jaxpr/ppermute | solution.py:14
  227.8 4.5 %fusion.43 = f32[2,16,16,768]{3,2,1,0:T(8,128)} fusion(bf16[2,16,16,1728]{3,2,1,0:T(8,128)(2,1)S(1)} %concatenate.36, bf16[1728,768,1,1]{1,0,3,2:T(8,128)(2,1)} %bitcast.34), kind=kOutput, calls=%fused_computation.49.clone.1 | convolution fusion | flops 1358954496 | bytes 5996544 | tf_op jit(solution)/shard_map/while/body/eval_jaxpr/dot_general | solution.py:28
  232.7 3.3 %pad_maximum_fusion.8 = (bf16[2,16,16,192]{3,2,1,0:T(8,128)(2,1)S(1)}, bf16[2,16,16,192]{3,2,1,0:T(8,128)(2,1)S(1)}, bf16[2,16,16,192]{3,2,1,0:T(8,128)(2,1)S(1)...) fusion(bf16[2,18,1,192]{3,2,1,0:T(2,128)(2,1)S(1)} %collective-per, ...), kind=kLoop, calls=%fused_computation.32.clone.1 | loop fusion | flops 2359296 | bytes 1428480 | tf_op jit(solution)/shard_map/while/body/eval_jaxpr/concatenate | solution.py:15
  238.5 3.9 %add_add_fusion.2 = f32[2,16,16,768]{3,2,1,0:T(8,128)S(1)} fusion(f32[2,16,16,768]{3,2,1,0:T(8,128)} %fusion.43, bf16[2,16,16,1728]{3,2,1,0:T(8,128)(2,1)S(1)} %concatenate.37, bf16[1728,768,1,1]{1,0,3,2:T(8,128)(2,1)} %bitcast.35, f32[768]{0:T(1024)S(1)} %get-tuple-element.219), kind=kOutput, calls=%fused_computation.clone.1 | convolution fusion | flops 1359740928 | bytes 7572480 | tf_op jit(solution)/shard_map/while/body/eval_jaxpr/dot_general | solution.py:28
  246.8 3.7 %collective-permute-start.1 = (bf16[2,1,16,192]{3,2,1,0:T(8,128)(2,1)S(1)}, bf16[2,1,16,192]{3,2,1,0:T(8,128)(2,1)S(1)}, u32[]{:S(2)}, u32[]{:S(2)}) collective-permute-start(bf16[2,1,16,192]{3,2,1,0:T(8,128)(2,1)S(1)} %get-tuple-element.179), channel_id=1, source_target_pairs={{0,1},{1,2},{2,3},{3,4},{4,5},{5,6},{6,7},{8,9},{9,10},{10,11},{11... | collective-permute-start | bytes 36872 | tf_op jit(solution)/shard_map/while/body/eval_jaxpr/ppermute | solution.py:13
  256.2 4.9 %collective-permute-start.2 = (bf16[2,18,1,192]{3,2,1,0:T(2,128)(2,1)S(1)}, bf16[2,18,1,192]{3,2,1,0:T(2,128)(2,1)S(1)}, u32[]{:S(2)}, u32[]{:S(2)}) collective-permute-start(bf16[2,18,1,192]{3,2,1,0:T(2,128)(2,1)S(1)} %get-tuple-element.181), channel_id=1, source_target_pairs={{8,0},{16,8},{24,16},{32,24},{40,32},{48,40},{56,48},{64,56},{72,6... | collective-permute-start | bytes 41480 | tf_op jit(solution)/shard_map/while/body/eval_jaxpr/ppermute | solution.py:14
  263.0 4.5 %fusion.43 = f32[2,16,16,768]{3,2,1,0:T(8,128)} fusion(bf16[2,16,16,1728]{3,2,1,0:T(8,128)(2,1)S(1)} %concatenate.36, bf16[1728,768,1,1]{1,0,3,2:T(8,128)(2,1)} %bitcast.34), kind=kOutput, calls=%fused_computation.49.clone.1 | convolution fusion | flops 1358954496 | bytes 5996544 | tf_op jit(solution)/shard_map/while/body/eval_jaxpr/dot_general | solution.py:28
  267.9 3.3 %pad_maximum_fusion.8 = (bf16[2,16,16,192]{3,2,1,0:T(8,128)(2,1)S(1)}, bf16[2,16,16,192]{3,2,1,0:T(8,128)(2,1)S(1)}, bf16[2,16,16,192]{3,2,1,0:T(8,128)(2,1)S(1)...) fusion(bf16[2,18,1,192]{3,2,1,0:T(2,128)(2,1)S(1)} %collective-per, ...), kind=kLoop, calls=%fused_computation.32.clone.1 | loop fusion | flops 2359296 | bytes 1428480 | tf_op jit(solution)/shard_map/while/body/eval_jaxpr/concatenate | solution.py:15
  273.7 3.9 %add_add_fusion.2 = f32[2,16,16,768]{3,2,1,0:T(8,128)S(1)} fusion(f32[2,16,16,768]{3,2,1,0:T(8,128)} %fusion.43, bf16[2,16,16,1728]{3,2,1,0:T(8,128)(2,1)S(1)} %concatenate.37, bf16[1728,768,1,1]{1,0,3,2:T(8,128)(2,1)} %bitcast.35, f32[768]{0:T(1024)S(1)} %get-tuple-element.219), kind=kOutput, calls=%fused_computation.clone.1 | convolution fusion | flops 1359740928 | bytes 7572480 | tf_op jit(solution)/shard_map/while/body/eval_jaxpr/dot_general | solution.py:28
  282.0 3.7 %collective-permute-start.1 = (bf16[2,1,16,192]{3,2,1,0:T(8,128)(2,1)S(1)}, bf16[2,1,16,192]{3,2,1,0:T(8,128)(2,1)S(1)}, u32[]{:S(2)}, u32[]{:S(2)}) collective-permute-start(bf16[2,1,16,192]{3,2,1,0:T(8,128)(2,1)S(1)} %get-tuple-element.179), channel_id=1, source_target_pairs={{0,1},{1,2},{2,3},{3,4},{4,5},{5,6},{6,7},{8,9},{9,10},{10,11},{11... | collective-permute-start | bytes 36872 | tf_op jit(solution)/shard_map/while/body/eval_jaxpr/ppermute | solution.py:13
  291.4 4.9 %collective-permute-start.2 = (bf16[2,18,1,192]{3,2,1,0:T(2,128)(2,1)S(1)}, bf16[2,18,1,192]{3,2,1,0:T(2,128)(2,1)S(1)}, u32[]{:S(2)}, u32[]{:S(2)}) collective-permute-start(bf16[2,18,1,192]{3,2,1,0:T(2,128)(2,1)S(1)} %get-tuple-element.181), channel_id=1, source_target_pairs={{8,0},{16,8},{24,16},{32,24},{40,32},{48,40},{56,48},{64,56},{72,6... | collective-permute-start | bytes 41480 | tf_op jit(solution)/shard_map/while/body/eval_jaxpr/ppermute | solution.py:14
  298.2 4.5 %fusion.43 = f32[2,16,16,768]{3,2,1,0:T(8,128)} fusion(bf16[2,16,16,1728]{3,2,1,0:T(8,128)(2,1)S(1)} %concatenate.36, bf16[1728,768,1,1]{1,0,3,2:T(8,128)(2,1)} %bitcast.34), kind=kOutput, calls=%fused_computation.49.clone.1 | convolution fusion | flops 1358954496 | bytes 5996544 | tf_op jit(solution)/shard_map/while/body/eval_jaxpr/dot_general | solution.py:28
  303.1 3.3 %pad_maximum_fusion.8 = (bf16[2,16,16,192]{3,2,1,0:T(8,128)(2,1)S(1)}, bf16[2,16,16,192]{3,2,1,0:T(8,128)(2,1)S(1)}, bf16[2,16,16,192]{3,2,1,0:T(8,128)(2,1)S(1)...) fusion(bf16[2,18,1,192]{3,2,1,0:T(2,128)(2,1)S(1)} %collective-per, ...), kind=kLoop, calls=%fused_computation.32.clone.1 | loop fusion | flops 2359296 | bytes 1428480 | tf_op jit(solution)/shard_map/while/body/eval_jaxpr/concatenate | solution.py:15
  308.9 3.9 %add_add_fusion.2 = f32[2,16,16,768]{3,2,1,0:T(8,128)S(1)} fusion(f32[2,16,16,768]{3,2,1,0:T(8,128)} %fusion.43, bf16[2,16,16,1728]{3,2,1,0:T(8,128)(2,1)S(1)} %concatenate.37, bf16[1728,768,1,1]{1,0,3,2:T(8,128)(2,1)} %bitcast.35, f32[768]{0:T(1024)S(1)} %get-tuple-element.219), kind=kOutput, calls=%fused_computation.clone.1 | convolution fusion | flops 1359740928 | bytes 7572480 | tf_op jit(solution)/shard_map/while/body/eval_jaxpr/dot_general | solution.py:28
  (193 shorter events, 124.7 us)
Async XLA Ops:
  0.6 8.7 %copy-start.5 = (bf16[8,2,16,16,192]{4,3,2,1,0:T(8,128)(2,1)S(1)}, bf16[8,2,16,16,192]{4,3,2,1,0:T(8,128)(2,1)}, u32[]{:S(2)}) copy-start(bf16[8,2,16,16,192]{4,3,2,1,0:T(8,128)(2,1)} %param.8) | copy-start | bytes 4718596
  3.6 5.6 %collective-permute-start.4 = (bf16[8,2,1,16,192]{4,3,2,1,0:T(8,128)(2,1)S(1)}, bf16[8,2,1,16,192]{4,3,2,1,0:T(8,128)(2,1)S(1)}, u32[]{:S(2)}, u32[]{:S(2)}) collective-permute-start(bf16[8,2,1,16,192]{4,3,2,1,0:T(8,128)(2,1)S(1)} %get-tuple-element.94), channel_id=1, source_target_pairs={{0,1},{1,2},{2,3},{3,4},{4,5},{5,6},{6,7},{8,9},{9,10},{10,11},{11... | collective-permute-start | bytes 294920 | tf_op jit(solution)/shard_map/ppermute | solution.py:13
  7.3 6.3 %collective-permute-start.5 = (bf16[8,2,1,16,192]{4,3,2,1,0:T(8,128)(2,1)S(1)}, bf16[8,2,1,16,192]{4,3,2,1,0:T(8,128)(2,1)S(1)}, u32[]{:S(2)}, u32[]{:S(2)}) collective-permute-start(bf16[8,2,1,16,192]{4,3,2,1,0:T(8,128)(2,1)S(1)} %get-tuple-element.93), channel_id=1, source_target_pairs={{1,0},{2,1},{3,2},{4,3},{5,4},{6,5},{7,6},{9,8},{10,9},{11,10},{12... | collective-permute-start | bytes 294920 | tf_op jit(solution)/shard_map/ppermute | solution.py:14
  13.6 1.4 copy-start.4
  15.5 9.1 %collective-permute-start.7 = (bf16[8,2,18,1,192]{4,3,2,1,0:T(2,128)(2,1)S(1)}, bf16[8,2,18,1,192]{4,3,2,1,0:T(2,128)(2,1)S(1)}, u32[]{:S(2)}, u32[]{:S(2)}) collective-permute-start(bf16[8,2,18,1,192]{4,3,2,1,0:T(2,128)(2,1)S(1)} %get-tuple-element.92), channel_id=1, source_target_pairs={{8,0},{16,8},{24,16},{32,24},{40,32},{48,40},{56,48},{64,56},{72,6... | collective-permute-start | bytes 331784 | tf_op jit(solution)/shard_map/ppermute | solution.py:14
  20.0 10.8 %collective-permute-start.6 = (bf16[8,2,18,1,192]{4,3,2,1,0:T(2,128)(2,1)S(1)}, bf16[8,2,18,1,192]{4,3,2,1,0:T(2,128)(2,1)S(1)}, u32[]{:S(2)}, u32[]{:S(2)}) collective-permute-start(bf16[8,2,18,1,192]{4,3,2,1,0:T(2,128)(2,1)S(1)} %get-tuple-element.91), channel_id=1, source_target_pairs={{0,8},{8,16},{16,24},{24,32},{32,40},{40,48},{48,56},{56,64},{64,7... | collective-permute-start | bytes 331784 | tf_op jit(solution)/shard_map/ppermute | solution.py:13
  21.9 13.7 %copy-start = (bf16[2,16,16,192]{3,2,1,0:T(8,128)(2,1)S(1)}, bf16[2,16,16,192]{3,2,1,0:T(8,128)(2,1)}, u32[]{:S(2)}) copy-start(bf16[2,16,16,192]{3,2,1,0:T(8,128)(2,1)} %param.12) | copy-start | bytes 589828
  22.0 13.7 %copy-start.6 = (f32[768]{0:T(1024)S(1)}, f32[768]{0:T(1024)}, u32[]{:S(2)}) copy-start(f32[768]{0:T(1024)} %param.11) | copy-start | bytes 9220
  35.7 11.4 %collective-permute-start = (bf16[2,1,16,192]{3,2,1,0:T(8,128)(2,1)S(1)}, bf16[2,1,16,192]{3,2,1,0:T(8,128)(2,1)S(1)}, u32[]{:S(2)}, u32[]{:S(2)}) collective-permute-start(bf16[2,1,16,192]{3,2,1,0:T(8,128)(2,1)S(1)} %get-tuple-element.178), channel_id=1, source_target_pairs={{1,0},{2,1},{3,2},{4,3},{5,4},{6,5},{7,6},{9,8},{10,9},{11,10},{12... | collective-permute-start | bytes 36872 | tf_op jit(solution)/shard_map/while/body/eval_jaxpr/ppermute | solution.py:14
  37.6 9.5 %collective-permute-start.1 = (bf16[2,1,16,192]{3,2,1,0:T(8,128)(2,1)S(1)}, bf16[2,1,16,192]{3,2,1,0:T(8,128)(2,1)S(1)}, u32[]{:S(2)}, u32[]{:S(2)}) collective-permute-start(bf16[2,1,16,192]{3,2,1,0:T(8,128)(2,1)S(1)} %get-tuple-element.179), channel_id=1, source_target_pairs={{0,1},{1,2},{2,3},{3,4},{4,5},{5,6},{6,7},{8,9},{9,10},{10,11},{11... | collective-permute-start | bytes 36872 | tf_op jit(solution)/shard_map/while/body/eval_jaxpr/ppermute | solution.py:13
  48.0 9.8 %collective-permute-start.2 = (bf16[2,18,1,192]{3,2,1,0:T(2,128)(2,1)S(1)}, bf16[2,18,1,192]{3,2,1,0:T(2,128)(2,1)S(1)}, u32[]{:S(2)}, u32[]{:S(2)}) collective-permute-start(bf16[2,18,1,192]{3,2,1,0:T(2,128)(2,1)S(1)} %get-tuple-element.181), channel_id=1, source_target_pairs={{8,0},{16,8},{24,16},{32,24},{40,32},{48,40},{56,48},{64,56},{72,6... | collective-permute-start | bytes 41480 | tf_op jit(solution)/shard_map/while/body/eval_jaxpr/ppermute | solution.py:14
  49.9 7.9 %collective-permute-start.3 = (bf16[2,18,1,192]{3,2,1,0:T(2,128)(2,1)S(1)}, bf16[2,18,1,192]{3,2,1,0:T(2,128)(2,1)S(1)}, u32[]{:S(2)}, u32[]{:S(2)}) collective-permute-start(bf16[2,18,1,192]{3,2,1,0:T(2,128)(2,1)S(1)} %get-tuple-element.182), channel_id=1, source_target_pairs={{0,8},{8,16},{16,24},{24,32},{32,40},{40,48},{48,56},{56,64},{64,7... | collective-permute-start | bytes 41480 | tf_op jit(solution)/shard_map/while/body/eval_jaxpr/ppermute | solution.py:13
  63.6 3.9 %copy-start.1 = (f32[2,16,16,192]{3,2,1,0:T(8,128)S(1)}, f32[2,16,16,192]{3,2,1,0:T(8,128)}, u32[]{:S(2)}) copy-start(f32[2,16,16,192]{3,2,1,0:T(8,128)} %get-tuple-element.205) | copy-start | bytes 1179652 | tf_op jit(solution)/shard_map/while
  69.8 10.4 %collective-permute-start = (bf16[2,1,16,192]{3,2,1,0:T(8,128)(2,1)S(1)}, bf16[2,1,16,192]{3,2,1,0:T(8,128)(2,1)S(1)}, u32[]{:S(2)}, u32[]{:S(2)}) collective-permute-start(bf16[2,1,16,192]{3,2,1,0:T(8,128)(2,1)S(1)} %get-tuple-element.178), channel_id=1, source_target_pairs={{1,0},{2,1},{3,2},{4,3},{5,4},{6,5},{7,6},{9,8},{10,9},{11,10},{12... | collective-permute-start | bytes 36872 | tf_op jit(solution)/shard_map/while/body/eval_jaxpr/ppermute | solution.py:14
  71.7 8.4 %collective-permute-start.1 = (bf16[2,1,16,192]{3,2,1,0:T(8,128)(2,1)S(1)}, bf16[2,1,16,192]{3,2,1,0:T(8,128)(2,1)S(1)}, u32[]{:S(2)}, u32[]{:S(2)}) collective-permute-start(bf16[2,1,16,192]{3,2,1,0:T(8,128)(2,1)S(1)} %get-tuple-element.179), channel_id=1, source_target_pairs={{0,1},{1,2},{2,3},{3,4},{4,5},{5,6},{6,7},{8,9},{9,10},{10,11},{11... | collective-permute-start | bytes 36872 | tf_op jit(solution)/shard_map/while/body/eval_jaxpr/ppermute | solution.py:13
  81.1 10.5 %collective-permute-start.2 = (bf16[2,18,1,192]{3,2,1,0:T(2,128)(2,1)S(1)}, bf16[2,18,1,192]{3,2,1,0:T(2,128)(2,1)S(1)}, u32[]{:S(2)}, u32[]{:S(2)}) collective-permute-start(bf16[2,18,1,192]{3,2,1,0:T(2,128)(2,1)S(1)} %get-tuple-element.181), channel_id=1, source_target_pairs={{8,0},{16,8},{24,16},{32,24},{40,32},{48,40},{56,48},{64,56},{72,6... | collective-permute-start | bytes 41480 | tf_op jit(solution)/shard_map/while/body/eval_jaxpr/ppermute | solution.py:14
  85.1 6.8 %collective-permute-start.3 = (bf16[2,18,1,192]{3,2,1,0:T(2,128)(2,1)S(1)}, bf16[2,18,1,192]{3,2,1,0:T(2,128)(2,1)S(1)}, u32[]{:S(2)}, u32[]{:S(2)}) collective-permute-start(bf16[2,18,1,192]{3,2,1,0:T(2,128)(2,1)S(1)} %get-tuple-element.182), channel_id=1, source_target_pairs={{0,8},{8,16},{16,24},{24,32},{32,40},{40,48},{48,56},{56,64},{64,7... | collective-permute-start | bytes 41480 | tf_op jit(solution)/shard_map/while/body/eval_jaxpr/ppermute | solution.py:13
  97.8 3.9 %copy-start.1 = (f32[2,16,16,192]{3,2,1,0:T(8,128)S(1)}, f32[2,16,16,192]{3,2,1,0:T(8,128)}, u32[]{:S(2)}) copy-start(f32[2,16,16,192]{3,2,1,0:T(8,128)} %get-tuple-element.205) | copy-start | bytes 1179652 | tf_op jit(solution)/shard_map/while
  103.9 10.6 %collective-permute-start = (bf16[2,1,16,192]{3,2,1,0:T(8,128)(2,1)S(1)}, bf16[2,1,16,192]{3,2,1,0:T(8,128)(2,1)S(1)}, u32[]{:S(2)}, u32[]{:S(2)}) collective-permute-start(bf16[2,1,16,192]{3,2,1,0:T(8,128)(2,1)S(1)} %get-tuple-element.178), channel_id=1, source_target_pairs={{1,0},{2,1},{3,2},{4,3},{5,4},{6,5},{7,6},{9,8},{10,9},{11,10},{12... | collective-permute-start | bytes 36872 | tf_op jit(solution)/shard_map/while/body/eval_jaxpr/ppermute | solution.py:14
  106.1 8.5 %collective-permute-start.1 = (bf16[2,1,16,192]{3,2,1,0:T(8,128)(2,1)S(1)}, bf16[2,1,16,192]{3,2,1,0:T(8,128)(2,1)S(1)}, u32[]{:S(2)}, u32[]{:S(2)}) collective-permute-start(bf16[2,1,16,192]{3,2,1,0:T(8,128)(2,1)S(1)} %get-tuple-element.179), channel_id=1, source_target_pairs={{0,1},{1,2},{2,3},{3,4},{4,5},{5,6},{6,7},{8,9},{9,10},{10,11},{11... | collective-permute-start | bytes 36872 | tf_op jit(solution)/shard_map/while/body/eval_jaxpr/ppermute | solution.py:13
  115.5 11.3 %collective-permute-start.2 = (bf16[2,18,1,192]{3,2,1,0:T(2,128)(2,1)S(1)}, bf16[2,18,1,192]{3,2,1,0:T(2,128)(2,1)S(1)}, u32[]{:S(2)}, u32[]{:S(2)}) collective-permute-start(bf16[2,18,1,192]{3,2,1,0:T(2,128)(2,1)S(1)} %get-tuple-element.181), channel_id=1, source_target_pairs={{8,0},{16,8},{24,16},{32,24},{40,32},{48,40},{56,48},{64,56},{72,6... | collective-permute-start | bytes 41480 | tf_op jit(solution)/shard_map/while/body/eval_jaxpr/ppermute | solution.py:14
  120.3 6.8 %collective-permute-start.3 = (bf16[2,18,1,192]{3,2,1,0:T(2,128)(2,1)S(1)}, bf16[2,18,1,192]{3,2,1,0:T(2,128)(2,1)S(1)}, u32[]{:S(2)}, u32[]{:S(2)}) collective-permute-start(bf16[2,18,1,192]{3,2,1,0:T(2,128)(2,1)S(1)} %get-tuple-element.182), channel_id=1, source_target_pairs={{0,8},{8,16},{16,24},{24,32},{32,40},{40,48},{48,56},{56,64},{64,7... | collective-permute-start | bytes 41480 | tf_op jit(solution)/shard_map/while/body/eval_jaxpr/ppermute | solution.py:13
  132.9 3.9 %copy-start.1 = (f32[2,16,16,192]{3,2,1,0:T(8,128)S(1)}, f32[2,16,16,192]{3,2,1,0:T(8,128)}, u32[]{:S(2)}) copy-start(f32[2,16,16,192]{3,2,1,0:T(8,128)} %get-tuple-element.205) | copy-start | bytes 1179652 | tf_op jit(solution)/shard_map/while
  139.1 10.6 %collective-permute-start = (bf16[2,1,16,192]{3,2,1,0:T(8,128)(2,1)S(1)}, bf16[2,1,16,192]{3,2,1,0:T(8,128)(2,1)S(1)}, u32[]{:S(2)}, u32[]{:S(2)}) collective-permute-start(bf16[2,1,16,192]{3,2,1,0:T(8,128)(2,1)S(1)} %get-tuple-element.178), channel_id=1, source_target_pairs={{1,0},{2,1},{3,2},{4,3},{5,4},{6,5},{7,6},{9,8},{10,9},{11,10},{12... | collective-permute-start | bytes 36872 | tf_op jit(solution)/shard_map/while/body/eval_jaxpr/ppermute | solution.py:14
  141.2 8.5 %collective-permute-start.1 = (bf16[2,1,16,192]{3,2,1,0:T(8,128)(2,1)S(1)}, bf16[2,1,16,192]{3,2,1,0:T(8,128)(2,1)S(1)}, u32[]{:S(2)}, u32[]{:S(2)}) collective-permute-start(bf16[2,1,16,192]{3,2,1,0:T(8,128)(2,1)S(1)} %get-tuple-element.179), channel_id=1, source_target_pairs={{0,1},{1,2},{2,3},{3,4},{4,5},{5,6},{6,7},{8,9},{9,10},{10,11},{11... | collective-permute-start | bytes 36872 | tf_op jit(solution)/shard_map/while/body/eval_jaxpr/ppermute | solution.py:13
  150.7 11.3 %collective-permute-start.2 = (bf16[2,18,1,192]{3,2,1,0:T(2,128)(2,1)S(1)}, bf16[2,18,1,192]{3,2,1,0:T(2,128)(2,1)S(1)}, u32[]{:S(2)}, u32[]{:S(2)}) collective-permute-start(bf16[2,18,1,192]{3,2,1,0:T(2,128)(2,1)S(1)} %get-tuple-element.181), channel_id=1, source_target_pairs={{8,0},{16,8},{24,16},{32,24},{40,32},{48,40},{56,48},{64,56},{72,6... | collective-permute-start | bytes 41480 | tf_op jit(solution)/shard_map/while/body/eval_jaxpr/ppermute | solution.py:14
  155.5 6.8 %collective-permute-start.3 = (bf16[2,18,1,192]{3,2,1,0:T(2,128)(2,1)S(1)}, bf16[2,18,1,192]{3,2,1,0:T(2,128)(2,1)S(1)}, u32[]{:S(2)}, u32[]{:S(2)}) collective-permute-start(bf16[2,18,1,192]{3,2,1,0:T(2,128)(2,1)S(1)} %get-tuple-element.182), channel_id=1, source_target_pairs={{0,8},{8,16},{16,24},{24,32},{32,40},{40,48},{48,56},{56,64},{64,7... | collective-permute-start | bytes 41480 | tf_op jit(solution)/shard_map/while/body/eval_jaxpr/ppermute | solution.py:13
  168.1 3.9 %copy-start.1 = (f32[2,16,16,192]{3,2,1,0:T(8,128)S(1)}, f32[2,16,16,192]{3,2,1,0:T(8,128)}, u32[]{:S(2)}) copy-start(f32[2,16,16,192]{3,2,1,0:T(8,128)} %get-tuple-element.205) | copy-start | bytes 1179652 | tf_op jit(solution)/shard_map/while
  174.3 10.6 %collective-permute-start = (bf16[2,1,16,192]{3,2,1,0:T(8,128)(2,1)S(1)}, bf16[2,1,16,192]{3,2,1,0:T(8,128)(2,1)S(1)}, u32[]{:S(2)}, u32[]{:S(2)}) collective-permute-start(bf16[2,1,16,192]{3,2,1,0:T(8,128)(2,1)S(1)} %get-tuple-element.178), channel_id=1, source_target_pairs={{1,0},{2,1},{3,2},{4,3},{5,4},{6,5},{7,6},{9,8},{10,9},{11,10},{12... | collective-permute-start | bytes 36872 | tf_op jit(solution)/shard_map/while/body/eval_jaxpr/ppermute | solution.py:14
  176.4 8.5 %collective-permute-start.1 = (bf16[2,1,16,192]{3,2,1,0:T(8,128)(2,1)S(1)}, bf16[2,1,16,192]{3,2,1,0:T(8,128)(2,1)S(1)}, u32[]{:S(2)}, u32[]{:S(2)}) collective-permute-start(bf16[2,1,16,192]{3,2,1,0:T(8,128)(2,1)S(1)} %get-tuple-element.179), channel_id=1, source_target_pairs={{0,1},{1,2},{2,3},{3,4},{4,5},{5,6},{6,7},{8,9},{9,10},{10,11},{11... | collective-permute-start | bytes 36872 | tf_op jit(solution)/shard_map/while/body/eval_jaxpr/ppermute | solution.py:13
  185.9 11.3 %collective-permute-start.2 = (bf16[2,18,1,192]{3,2,1,0:T(2,128)(2,1)S(1)}, bf16[2,18,1,192]{3,2,1,0:T(2,128)(2,1)S(1)}, u32[]{:S(2)}, u32[]{:S(2)}) collective-permute-start(bf16[2,18,1,192]{3,2,1,0:T(2,128)(2,1)S(1)} %get-tuple-element.181), channel_id=1, source_target_pairs={{8,0},{16,8},{24,16},{32,24},{40,32},{48,40},{56,48},{64,56},{72,6... | collective-permute-start | bytes 41480 | tf_op jit(solution)/shard_map/while/body/eval_jaxpr/ppermute | solution.py:14
  190.7 6.8 %collective-permute-start.3 = (bf16[2,18,1,192]{3,2,1,0:T(2,128)(2,1)S(1)}, bf16[2,18,1,192]{3,2,1,0:T(2,128)(2,1)S(1)}, u32[]{:S(2)}, u32[]{:S(2)}) collective-permute-start(bf16[2,18,1,192]{3,2,1,0:T(2,128)(2,1)S(1)} %get-tuple-element.182), channel_id=1, source_target_pairs={{0,8},{8,16},{16,24},{24,32},{32,40},{40,48},{48,56},{56,64},{64,7... | collective-permute-start | bytes 41480 | tf_op jit(solution)/shard_map/while/body/eval_jaxpr/ppermute | solution.py:13
  203.3 3.9 %copy-start.1 = (f32[2,16,16,192]{3,2,1,0:T(8,128)S(1)}, f32[2,16,16,192]{3,2,1,0:T(8,128)}, u32[]{:S(2)}) copy-start(f32[2,16,16,192]{3,2,1,0:T(8,128)} %get-tuple-element.205) | copy-start | bytes 1179652 | tf_op jit(solution)/shard_map/while
  209.5 10.6 %collective-permute-start = (bf16[2,1,16,192]{3,2,1,0:T(8,128)(2,1)S(1)}, bf16[2,1,16,192]{3,2,1,0:T(8,128)(2,1)S(1)}, u32[]{:S(2)}, u32[]{:S(2)}) collective-permute-start(bf16[2,1,16,192]{3,2,1,0:T(8,128)(2,1)S(1)} %get-tuple-element.178), channel_id=1, source_target_pairs={{1,0},{2,1},{3,2},{4,3},{5,4},{6,5},{7,6},{9,8},{10,9},{11,10},{12... | collective-permute-start | bytes 36872 | tf_op jit(solution)/shard_map/while/body/eval_jaxpr/ppermute | solution.py:14
  211.6 8.5 %collective-permute-start.1 = (bf16[2,1,16,192]{3,2,1,0:T(8,128)(2,1)S(1)}, bf16[2,1,16,192]{3,2,1,0:T(8,128)(2,1)S(1)}, u32[]{:S(2)}, u32[]{:S(2)}) collective-permute-start(bf16[2,1,16,192]{3,2,1,0:T(8,128)(2,1)S(1)} %get-tuple-element.179), channel_id=1, source_target_pairs={{0,1},{1,2},{2,3},{3,4},{4,5},{5,6},{6,7},{8,9},{9,10},{10,11},{11... | collective-permute-start | bytes 36872 | tf_op jit(solution)/shard_map/while/body/eval_jaxpr/ppermute | solution.py:13
  221.0 11.3 %collective-permute-start.2 = (bf16[2,18,1,192]{3,2,1,0:T(2,128)(2,1)S(1)}, bf16[2,18,1,192]{3,2,1,0:T(2,128)(2,1)S(1)}, u32[]{:S(2)}, u32[]{:S(2)}) collective-permute-start(bf16[2,18,1,192]{3,2,1,0:T(2,128)(2,1)S(1)} %get-tuple-element.181), channel_id=1, source_target_pairs={{8,0},{16,8},{24,16},{32,24},{40,32},{48,40},{56,48},{64,56},{72,6... | collective-permute-start | bytes 41480 | tf_op jit(solution)/shard_map/while/body/eval_jaxpr/ppermute | solution.py:14
  225.9 6.8 %collective-permute-start.3 = (bf16[2,18,1,192]{3,2,1,0:T(2,128)(2,1)S(1)}, bf16[2,18,1,192]{3,2,1,0:T(2,128)(2,1)S(1)}, u32[]{:S(2)}, u32[]{:S(2)}) collective-permute-start(bf16[2,18,1,192]{3,2,1,0:T(2,128)(2,1)S(1)} %get-tuple-element.182), channel_id=1, source_target_pairs={{0,8},{8,16},{16,24},{24,32},{32,40},{40,48},{48,56},{56,64},{64,7... | collective-permute-start | bytes 41480 | tf_op jit(solution)/shard_map/while/body/eval_jaxpr/ppermute | solution.py:13
  238.5 3.9 %copy-start.1 = (f32[2,16,16,192]{3,2,1,0:T(8,128)S(1)}, f32[2,16,16,192]{3,2,1,0:T(8,128)}, u32[]{:S(2)}) copy-start(f32[2,16,16,192]{3,2,1,0:T(8,128)} %get-tuple-element.205) | copy-start | bytes 1179652 | tf_op jit(solution)/shard_map/while
  244.7 10.6 %collective-permute-start = (bf16[2,1,16,192]{3,2,1,0:T(8,128)(2,1)S(1)}, bf16[2,1,16,192]{3,2,1,0:T(8,128)(2,1)S(1)}, u32[]{:S(2)}, u32[]{:S(2)}) collective-permute-start(bf16[2,1,16,192]{3,2,1,0:T(8,128)(2,1)S(1)} %get-tuple-element.178), channel_id=1, source_target_pairs={{1,0},{2,1},{3,2},{4,3},{5,4},{6,5},{7,6},{9,8},{10,9},{11,10},{12... | collective-permute-start | bytes 36872 | tf_op jit(solution)/shard_map/while/body/eval_jaxpr/ppermute | solution.py:14
  246.8 8.5 %collective-permute-start.1 = (bf16[2,1,16,192]{3,2,1,0:T(8,128)(2,1)S(1)}, bf16[2,1,16,192]{3,2,1,0:T(8,128)(2,1)S(1)}, u32[]{:S(2)}, u32[]{:S(2)}) collective-permute-start(bf16[2,1,16,192]{3,2,1,0:T(8,128)(2,1)S(1)} %get-tuple-element.179), channel_id=1, source_target_pairs={{0,1},{1,2},{2,3},{3,4},{4,5},{5,6},{6,7},{8,9},{9,10},{10,11},{11... | collective-permute-start | bytes 36872 | tf_op jit(solution)/shard_map/while/body/eval_jaxpr/ppermute | solution.py:13
  256.2 11.3 %collective-permute-start.2 = (bf16[2,18,1,192]{3,2,1,0:T(2,128)(2,1)S(1)}, bf16[2,18,1,192]{3,2,1,0:T(2,128)(2,1)S(1)}, u32[]{:S(2)}, u32[]{:S(2)}) collective-permute-start(bf16[2,18,1,192]{3,2,1,0:T(2,128)(2,1)S(1)} %get-tuple-element.181), channel_id=1, source_target_pairs={{8,0},{16,8},{24,16},{32,24},{40,32},{48,40},{56,48},{64,56},{72,6... | collective-permute-start | bytes 41480 | tf_op jit(solution)/shard_map/while/body/eval_jaxpr/ppermute | solution.py:14
  261.1 6.8 %collective-permute-start.3 = (bf16[2,18,1,192]{3,2,1,0:T(2,128)(2,1)S(1)}, bf16[2,18,1,192]{3,2,1,0:T(2,128)(2,1)S(1)}, u32[]{:S(2)}, u32[]{:S(2)}) collective-permute-start(bf16[2,18,1,192]{3,2,1,0:T(2,128)(2,1)S(1)} %get-tuple-element.182), channel_id=1, source_target_pairs={{0,8},{8,16},{16,24},{24,32},{32,40},{40,48},{48,56},{56,64},{64,7... | collective-permute-start | bytes 41480 | tf_op jit(solution)/shard_map/while/body/eval_jaxpr/ppermute | solution.py:13
  273.7 3.9 %copy-start.1 = (f32[2,16,16,192]{3,2,1,0:T(8,128)S(1)}, f32[2,16,16,192]{3,2,1,0:T(8,128)}, u32[]{:S(2)}) copy-start(f32[2,16,16,192]{3,2,1,0:T(8,128)} %get-tuple-element.205) | copy-start | bytes 1179652 | tf_op jit(solution)/shard_map/while
  279.9 10.6 %collective-permute-start = (bf16[2,1,16,192]{3,2,1,0:T(8,128)(2,1)S(1)}, bf16[2,1,16,192]{3,2,1,0:T(8,128)(2,1)S(1)}, u32[]{:S(2)}, u32[]{:S(2)}) collective-permute-start(bf16[2,1,16,192]{3,2,1,0:T(8,128)(2,1)S(1)} %get-tuple-element.178), channel_id=1, source_target_pairs={{1,0},{2,1},{3,2},{4,3},{5,4},{6,5},{7,6},{9,8},{10,9},{11,10},{12... | collective-permute-start | bytes 36872 | tf_op jit(solution)/shard_map/while/body/eval_jaxpr/ppermute | solution.py:14
  282.0 8.5 %collective-permute-start.1 = (bf16[2,1,16,192]{3,2,1,0:T(8,128)(2,1)S(1)}, bf16[2,1,16,192]{3,2,1,0:T(8,128)(2,1)S(1)}, u32[]{:S(2)}, u32[]{:S(2)}) collective-permute-start(bf16[2,1,16,192]{3,2,1,0:T(8,128)(2,1)S(1)} %get-tuple-element.179), channel_id=1, source_target_pairs={{0,1},{1,2},{2,3},{3,4},{4,5},{5,6},{6,7},{8,9},{9,10},{10,11},{11... | collective-permute-start | bytes 36872 | tf_op jit(solution)/shard_map/while/body/eval_jaxpr/ppermute | solution.py:13
  291.4 11.3 %collective-permute-start.2 = (bf16[2,18,1,192]{3,2,1,0:T(2,128)(2,1)S(1)}, bf16[2,18,1,192]{3,2,1,0:T(2,128)(2,1)S(1)}, u32[]{:S(2)}, u32[]{:S(2)}) collective-permute-start(bf16[2,18,1,192]{3,2,1,0:T(2,128)(2,1)S(1)} %get-tuple-element.181), channel_id=1, source_target_pairs={{8,0},{16,8},{24,16},{32,24},{40,32},{48,40},{56,48},{64,56},{72,6... | collective-permute-start | bytes 41480 | tf_op jit(solution)/shard_map/while/body/eval_jaxpr/ppermute | solution.py:14
  296.3 6.8 %collective-permute-start.3 = (bf16[2,18,1,192]{3,2,1,0:T(2,128)(2,1)S(1)}, bf16[2,18,1,192]{3,2,1,0:T(2,128)(2,1)S(1)}, u32[]{:S(2)}, u32[]{:S(2)}) collective-permute-start(bf16[2,18,1,192]{3,2,1,0:T(2,128)(2,1)S(1)} %get-tuple-element.182), channel_id=1, source_target_pairs={{0,8},{8,16},{16,24},{24,32},{32,40},{40,48},{48,56},{56,64},{64,7... | collective-permute-start | bytes 41480 | tf_op jit(solution)/shard_map/while/body/eval_jaxpr/ppermute | solution.py:13
  308.9 3.9 %copy-start.1 = (f32[2,16,16,192]{3,2,1,0:T(8,128)S(1)}, f32[2,16,16,192]{3,2,1,0:T(8,128)}, u32[]{:S(2)}) copy-start(f32[2,16,16,192]{3,2,1,0:T(8,128)} %get-tuple-element.205) | copy-start | bytes 1179652 | tf_op jit(solution)/shard_map/while
  (16 other events, 12.2 us)
where the time goes:
time: 320 us; the launch traced here: 315 us
  starting transfers between devices  111 us (35%)
  local copies, waits for them, and re-layouts  76.3 us (24%)
  matrix products  66.9 us (21%)
  other arithmetic  43.7 us (14%)
  waiting for transfers between devices  15.7 us (5%)
    dot_general x16, matrix products, conv_taps(): jnp.dot(flat_patches, flat_weights, preferred_element_type=jnp.float32)  66.9 us
    ppermute x18, starting transfers between devices, edge_swap(): from_next = lax.ppermute(low_edge, axis_label, up_pairs)  57.9 us
    ppermute x18, starting transfers between devices, edge_swap(): from_prev = lax.ppermute(high_edge, axis_label, down_pairs)  52.9 us
    concatenate x16, local copies, waits for them, and re-layouts, conv_taps(): patches = jnp.concatenate(tap_list, axis=-1)  40.8 us
    concatenate x17, other arithmetic, edge_swap(): return jnp.concatenate([from_prev, tile_arr, from_next], axis=split_dim)  31.7 us
    while x56, local copies, waits for them, and re-layouts  12.2 us
    dynamic_update_slice x8, other arithmetic, local_run(): final_pair, all_hidden = lax.scan(step_fn, (h_init, c_init), frames_ext)  12 us
    slice x8, local copies, waits for them, and re-layouts, conv_taps(): padded[:, row_off:row_off + out_rows, col_off:col_off + out_cols, :]  9.21 us
  transfers between devices with their start and end apart: 36, of which 10 were waited for; matrix products, arithmetic and copies ran while one was open for 24% of the time, Pallas kernels for 0%

commit v1 on v0

v1 whole, which is shorter than its diff:
```python
import functools

import jax
import jax.numpy as jnp
from jax import lax
from jax.experimental import pallas as pl
from jax.experimental.pallas import tpu as pltpu
from jax.sharding import PartitionSpec as P

MESH = pl.DeviceIdType.MESH
BF = jnp.bfloat16
F32 = jnp.float32

PITCH = 24
IMG_ROWS = 26
EXT_M = 336
DIRS = ((-1, 0), (1, 0), (0, -1), (0, 1), (-1, -1), (-1, 1), (1, -1), (1, 1))
OPP = (1, 0, 3, 2, 7, 6, 5, 4)


def cell(er, ec):
    return er * PITCH + ec


def corner_src(d):
    return (2 if DIRS[d][0] < 0 else 16), (2 if DIRS[d][1] < 0 else 16)


def corner_dst(d):
    return (18 if DIRS[d][0] < 0 else 0), (18 if DIRS[d][1] < 0 else 0)


def low_lanes(n):
    return lax.broadcasted_iota(jnp.int32, (n, 128), 1) < 64


def twice(v):
    return jnp.concatenate([v, v], axis=1)


def flat(img):
    return img.reshape(2, IMG_ROWS * PITCH, 128)


def put_col(img, er, ec, a, b):
    at = pl.ds(cell(er, ec), 16, stride=PITCH)
    flat(img)[0, at, :] = a
    flat(img)[1, at, :] = b


def get_col(img, lt, er, ec, n=16):
    return flat(img)[lt, pl.ds(cell(er, ec), n, stride=PITCH), :]


def put_rows(img, er, v):
    n = v.shape[0]
    v = v.reshape(n * 16, 192).astype(F32)
    img[0, pl.ds(er, n), 2:18, :] = v[:, :128].reshape(n, 16, 128)
    img[1, pl.ds(er, n), 2:18, :] = twice(v[:, 128:192]).reshape(n, 16, 128)


def build(img, tap, tail, strip, ext):
    first, n = (0, 20) if ext else (1, 18)
    lo = lax.broadcasted_iota(jnp.int32, (n, 16, 128), 2) < 64
    low = lax.broadcasted_iota(jnp.int32, (n - 2, 16, 128), 2) < 64
    for dc in range(3):
        tap[first:first + n, :, dc * 128:(dc + 1) * 128] = img[0, first:first + n, 1 + dc:17 + dc, :].astype(BF)
    b = [img[1, first:first + n, 1 + dc:17 + dc, :] for dc in range(3)]
    tap[first:first + n, :, 384:512] = jnp.where(lo, b[0], b[1]).astype(BF)
    m0, m1 = first * 16, (first + n - 2) * 16
    tail[m0:m1, 0:128] = jnp.where(low, b[2][0:n - 2], b[2][1:n - 1]).astype(BF).reshape(m1 - m0, 128)
    tail[m0:m1, 128:256] = b[2][2:n].astype(BF).reshape(m1 - m0, 128)
    if ext:
        lo24 = low_lanes(24)

        def both(f):
            return jnp.concatenate([f(1), f(18)], axis=0).astype(BF)

        for dr in range(3):
            for dc in range(3):
                strip[dr, :, dc * 128:(dc + 1) * 128] = both(lambda ec: get_col(img, 0, dr, ec + dc - 1, 24))
            strip[dr, :, 384:512] = both(lambda ec: jnp.where(lo24, get_col(img, 1, dr, ec - 1, 24), get_col(img, 1, dr, ec, 24)))
        tail[288:336, 0:128] = both(lambda ec: jnp.where(lo24, get_col(img, 1, 0, ec + 1, 24), get_col(img, 1, 1, ec + 1, 24)))
        tail[288:336, 128:256] = both(lambda ec: get_col(img, 1, 2, ec + 1, 24))


def conv(tap, tail, strip, w, ext):
    if ext:
        blocks = [jnp.concatenate([tap[dr:dr + 18].reshape(288, 512), strip[dr]], axis=0) for dr in range(3)]
        last = tail[:, 0:192]
    else:
        blocks = [tap[1 + dr:17 + dr].reshape(256, 512) for dr in range(3)]
        last = tail[16:272, 0:192]
    lhs = jnp.concatenate(blocks + [last], axis=1)
    return jnp.dot(lhs, w[...], preferred_element_type=F32)


def gates(z, c0, c1):
    n = c0.shape[0]
    lo = low_lanes(n)
    half = jnp.where(lo, 0.5, 1.0).astype(F32)
    off = jnp.where(lo, 0.5, 0.0).astype(F32)
    in0 = 0.5 * jnp.tanh(0.5 * z[0]) + 0.5
    a1 = 0.5 * jnp.tanh(0.5 * z[1]) + 0.5
    a2 = 0.5 * jnp.tanh(0.5 * z[2]) + 0.5
    out0 = 0.5 * jnp.tanh(0.5 * z[3]) + 0.5
    a4 = half * jnp.tanh(half * z[4]) + off
    a5 = jnp.tanh(z[5])
    forget0 = pltpu.roll(jnp.where(lo, a2, a1), 64, 1)
    cand0 = pltpu.roll(jnp.where(lo, a5, a4), 64, 1)
    in_forget1 = jnp.where(lo, a1, a2)
    out_cand1 = jnp.where(lo, a4, a5)
    c0n = forget0 * c0 + in0 * cand0
    prod = in_forget1 * jnp.where(lo, pltpu.roll(out_cand1, 64, 1), c1)
    c1n = prod + pltpu.roll(prod, 64, 1)
    h0 = out0 * jnp.tanh(c0n)
    h1 = out_cand1 * jnp.tanh(c1n)
    h1 = jnp.where(lo, h1, pltpu.roll(h1, 64, 1))
    return h0.astype(BF), h1.astype(BF), c0n, c1n


def kernel(frames, w_x, w_h, bias, h_init, c_init, h_all, c_final,
           fr, hin, cin, wx, wh, imgx, imgh, cst, tapx, tailx, stripx, taph, tailh, striph, gext, gpl, zbuf,
           s_xcol, s_xdiag, r_xrow, r_xcol, r_xdiag,
           s_hcol, s_ccol, s_diag, r_hrow, r_hcol, r_crow, r_ccol, r_diag,
           lsem, wsem, xs_sem, xr_sem, xd_s, xd_r, e_s, e_r, *, shape):
    n_rows, n_cols = shape
    row, col = lax.axis_index("rows"), lax.axis_index("cols")
    grp = lax.axis_index("batch")

    def has(d):
        dr, dc = DIRS[d]
        rr, cc = row + dr, col + dc
        return (rr >= 0) & (rr < n_rows) & (cc >= 0) & (cc < n_cols)

    def peer(d):
        return (grp, col + DIRS[d][1], row + DIRS[d][0])

    loads = [pltpu.make_async_copy(h_init, hin, lsem.at[0]), pltpu.make_async_copy(c_init, cin, lsem.at[1])]
    loads += [pltpu.make_async_copy(frames.at[pl.ds(2 * k, 2)], fr.at[pl.ds(2 * k, 2)], lsem.at[2 + k]) for k in range(4)]
    wloads = [[], []]
    for i, (src, dst) in enumerate(((w_x, wx), (w_h, wh))):
        n = 0
        for dr in range(3):
            for dc in range(3):
                at = dr * 512 + 384 + dc * 64 if dc < 2 else 1536 + dr * 64
                for c_at, rows_n, k_at in ((0, 128, dr * 512 + dc * 128), (128, 64, at)):
                    wloads[i].append(pltpu.make_async_copy(src.at[dr, dc, pl.ds(c_at, rows_n)], dst.at[pl.ds(k_at, rows_n)], wsem.at[i, n]))
                    n += 1
    for cp in loads[2:3] + loads[0:2] + loads[3:4] + wloads[0] + wloads[1] + loads[4:]:
        cp.start()

    barrier = pltpu.get_barrier_semaphore()
    for d in range(8):
        @pl.when(has(d))
        def _(d=d):
            pl.semaphore_signal(barrier, inc=1, device_id=peer(d), device_id_type=MESH)

    for d in range(8):
        @pl.when(jnp.logical_not(has(OPP[d])))
        def _(d=d):
            if d < 2:
                for ref in (r_xrow, r_hrow, r_crow):
                    ref[:, d] = jnp.zeros((ref.shape[0],) + ref.shape[2:], ref.dtype)
            elif d < 4:
                for ref in (r_xcol, r_hcol, r_ccol):
                    ref[:, d - 2] = jnp.zeros((ref.shape[0],) + ref.shape[2:], ref.dtype)
            else:
                for ref in (r_xdiag, r_diag):
                    ref[:, d - 4] = jnp.zeros((ref.shape[0],) + ref.shape[2:], ref.dtype)

    def frame_image(f, s):
        img = imgx.at[2 * f + s]
        put_rows(img, 2, fr[f, s])

    def frame_stage(k, s):
        for odd in range(2):
            f = 2 * k + odd
            img = imgx.at[2 * f + s]
            for side in range(2):
                for j in range(1 if odd else 2):
                    ec = (2 + j) if side == 0 else (17 - j)
                    s_xcol[f, side, j, s, :, 0:128] = get_col(img, 0, 2, ec).astype(BF)
                    s_xcol[f, side, j, s, :, 128:256] = get_col(img, 1, 2, ec).astype(BF)
            for d in range(4, 8):
                er, ec = corner_src(d)
                for lt in range(2):
                    if odd:
                        er1, ec1 = (2 if er == 2 else 17), (2 if ec == 2 else 17)
                        s_xdiag[k, d - 4, s, lt, 4:5, :] = img[lt, er1, pl.ds(ec1, 1), :]
                    else:
                        for i in range(2):
                            s_xdiag[k, d - 4, s, lt, 2 * i:2 * i + 2, :] = img[lt, er + i, pl.ds(ec, 2), :]

    def frame_copy(f, odd, d):
        if d < 2:
            at = (0 if d == 0 else 15) if odd else (0 if d == 0 else 14)
            src = fr.at[f, :, pl.ds(at, 1 if odd else 2)]
            dst = r_xrow.at[f, d, :, pl.ds(d if odd else 0, 1 if odd else 2)]
        else:
            src = s_xcol.at[f, d - 2, pl.ds(0, 1 if odd else 2)]
            dst = r_xcol.at[f, d - 2, pl.ds(0, 1 if odd else 2)]
        return pltpu.make_async_remote_copy(src_ref=src, dst_ref=dst, send_sem=xs_sem.at[f, d], recv_sem=xr_sem.at[f, d], device_id=peer(d), device_id_type=MESH)

    def frame_diag(k, d):
        return pltpu.make_async_remote_copy(src_ref=s_xdiag.at[k, d - 4], dst_ref=r_xdiag.at[k, d - 4], send_sem=xd_s.at[k, d - 4], recv_sem=xd_r.at[k, d - 4], device_id=peer(d), device_id_type=MESH)

    def frame_send(k, odd):
        for d in range(4):
            @pl.when(has(d))
            def _(d=d):
                frame_copy(2 * k + odd, odd, d).start()
        if not odd:
            for d in range(4, 8):
                @pl.when(has(d))
                def _(d=d):
                    frame_diag(k, d).start()

    def frame_wait(k):
        for d in range(8):
            @pl.when(has(OPP[d]))
            def _(d=d):
                if d < 4:
                    frame_copy(2 * k, 0, d).wait_recv()
                    frame_copy(2 * k + 1, 1, d).wait_recv()
                else:
                    frame_diag(k, d).wait_recv()
        for d in range(8):
            @pl.when(has(d))
            def _(d=d):
                if d < 4:
                    frame_copy(2 * k, 0, d).wait_send()
                    frame_copy(2 * k + 1, 1, d).wait_send()
                else:
                    frame_diag(k, d).wait_send()

    def frame_fill(k, odd, s):
        f = 2 * k + odd
        img = imgx.at[2 * f + s]
        for d in range(2):
            i, n = (d, 1) if odd else (0, 2)
            put_rows(img, (18 + i) if d == 0 else i, r_xrow[f, d, s, pl.ds(i, n)])
            for j in range(1 if odd else 2):
                v = r_xcol[f, d, j, s].astype(F32)
                put_col(img, 2, (18 + j) if d == 0 else (1 - j), v[:, 0:128], v[:, 128:256])
        for d in range(4, 8):
            er, ec = corner_dst(d)
            for lt in range(2):
                if odd:
                    er1, ec1 = (18 if er == 18 else 1), (18 if ec == 18 else 1)
                    img[lt, er1, pl.ds(ec1, 1), :] = r_xdiag[k, d - 4, s, lt, 4:5, :]
                else:
                    for i in range(2):
                        img[lt, er + i, pl.ds(ec, 2), :] = r_xdiag[k, d - 4, s, lt, 2 * i:2 * i + 2, :]

    def x_part(k, odd, s):
        img = imgx.at[2 * (2 * k + odd) + s]
        build(img, tapx.at[odd], tailx.at[odd], stripx, not odd)
        z = conv(tapx.at[odd], tailx.at[odd], stripx, wx, not odd)
        if odd:
            gpl[s] = z + bias[...]
        else:
            gext[s] = z + bias[...]

    def state_copies(e, s, d, hsrc):
        x = 2 * e + s

        def mk(src, dst, n):
            return pltpu.make_async_remote_copy(src_ref=src, dst_ref=dst, send_sem=e_s.at[x, n], recv_sem=e_r.at[x, n], device_id=peer(d), device_id_type=MESH)

        if d < 2:
            return [mk(hsrc.at[pl.ds(0 if d == 0 else 14, 2)], r_hrow.at[x, d], d),
                    mk(cst.at[s, :, pl.ds(16 if d == 0 else 256, 16)], r_crow.at[x, d], 8 + d)]
        if d < 4:
            return [mk(s_hcol.at[s, d - 2], r_hcol.at[x, d - 2], d), mk(s_ccol.at[s, d - 2], r_ccol.at[x, d - 2], 8 + d)]
        return [mk(s_diag.at[s, d - 4], r_diag.at[x, d - 4], d)]

    def state_stage(s):
        img = imgh.at[s]
        for side in range(2):
            for j in range(2):
                ec = (2 + j) if side == 0 else (17 - j)
                s_hcol[s, side, j, :, 0:128] = get_col(img, 0, 2, ec).astype(BF)
                s_hcol[s, side, j, :, 128:256] = get_col(img, 1, 2, ec).astype(BF)
            for lt in range(2):
                s_ccol[s, side, lt] = cst[s, lt, pl.ds(16 + 15 * side, 16, stride=16), :]
        for d in range(4, 8):
            er, ec = corner_src(d)
            er1, ec1 = (2 if er == 2 else 17), (2 if ec == 2 else 17)
            for lt in range(2):
                for i in range(2):
                    s_diag[s, d - 4, lt, 2 * i:2 * i + 2, :] = img[lt, er + i, pl.ds(ec, 2), :]
                s_diag[s, d - 4, lt, 4:5, :] = cst[s, lt, pl.ds((er1 - 1) * 16 + ec1 - 2, 1), :]

    def state_send(e, s, hsrc):
        for d in (2, 3, 4, 5, 6, 7, 0, 1):
            @pl.when(has(d))
            def _(d=d):
                for cp in state_copies(e, s, d, hsrc):
                    cp.start()

    def state_wait(e, s, hsrc):
        for d in range(8):
            @pl.when(has(OPP[d]))
            def _(d=d):
                for cp in state_copies(e, s, d, hsrc):
                    cp.wait_recv()
        for d in range(8):
            @pl.when(has(d))
            def _(d=d):
                for cp in state_copies(e, s, d, hsrc):
                    cp.wait_send()

    def state_fill(e, s):
        img = imgh.at[s]
        x = 2 * e + s
        for d in range(2):
            put_rows(img, 18 if d == 0 else 0, r_hrow[x, d])
            for lt in range(2):
                m = 272 if d == 0 else 0
                cst[s, lt, m:m + 16, :] = r_crow[x, d, lt]
            for j in range(2):
                v = r_hcol[x, d, j].astype(F32)
                put_col(img, 2, (18 + j) if d == 0 else (1 - j), v[:, 0:128], v[:, 128:256])
            for lt in range(2):
                m = 288 + (24 if d == 0 else 0) + 1
                cst[s, lt, pl.ds(m, 16), :] = r_ccol[x, d, lt]
        for d in range(4, 8):
            er, ec = corner_dst(d)
            m = 288 + (24 if ec == 18 else 0) + (17 if er == 18 else 0)
            for lt in range(2):
                for i in range(2):
                    img[lt, er + i, pl.ds(ec, 2), :] = r_diag[x, d - 4, lt, 2 * i:2 * i + 2, :]
                cst[s, lt, pl.ds(m, 1), :] = r_diag[x, d - 4, lt, 4:5, :]

    def flag(cond, n):
        return jnp.full((n, 128), jnp.where(cond, 1, 0).astype(jnp.int32)) > 0

    def update(s, t, ext, last=False):
        img = imgh.at[s]

        def unit(er, _):
            m = pl.multiple_of((er - 1) * 16, 16)
            zm = m if ext else pl.multiple_of(m - 16, 16)
            z = [zbuf[pl.ds(zm, 16), n * 128:(n + 1) * 128] for n in range(6)]
            h0, h1, c0, c1 = gates(z, cst[s, 0, pl.ds(m, 16), :], cst[s, 1, pl.ds(m, 16), :])
            cst[s, 0, pl.ds(m, 16), :] = c0
            cst[s, 1, pl.ds(m, 16), :] = c1
            f0, f1 = h0.astype(F32), h1.astype(F32)
            if ext:
                ok = flag(((er > 1) | has(0)) & ((er < 18) | has(1)), 16)
                f0, f1 = jnp.where(ok, f0, 0.0), jnp.where(ok, f1, 0.0)
            img[0, er, 2:18, :] = f0
            img[1, er, 2:18, :] = f1
            return 0

        lax.fori_loop(*((1, 19) if ext else (2, 18)), unit, 0)
        h_all[t, s, :, :, 0:128] = img[0, 2:18, 2:18, :].astype(BF)
        h_all[t, s, :, :, 128:192] = img[1, 2:18, 2:18, :].astype(BF)[:, :, 0:64]
        if last:
            c_final[s, :, :, 0:128] = cst[s, 0, 16:272, :].reshape(16, 16, 128)
            c_final[s, :, :, 128:192] = cst[s, 1, 16:272, :].reshape(16, 16, 128)[:, :, 0:64]
        if not ext:
            return
        pos = lax.broadcasted_iota(jnp.int32, (24, 128), 0)
        for side in range(2):
            ok = flag(has(2 + side), 24) & (flag(has(0), 24) | (pos > 0)) & (flag(has(1), 24) | (pos < 17))
            m = 288 + 24 * side
            z = [zbuf[m:m + 24, n * 128:(n + 1) * 128] for n in range(6)]
            h0, h1, c0, c1 = gates(z, cst[s, 0, m:m + 24, :], cst[s, 1, m:m + 24, :])
            f0, f1 = jnp.where(ok, h0.astype(F32), 0.0), jnp.where(ok, h1.astype(F32), 0.0)
            at = pl.ds(cell(1, 1 + 17 * side), 24, stride=PITCH)
            flat(img)[0, at, :] = f0
            flat(img)[1, at, :] = f1

    def h_step(s, t, ext, last=False):
        build(imgh.at[s], taph, tailh, striph, ext)
        z = conv(taph, tailh, striph, wh, ext)
        if ext:
            zbuf[...] = z + gext[s]
        else:
            zbuf[0:256, :] = z + gpl[s]
        update(s, t, ext, last)

    loads[2].wait()

    def first_frames(s, _):
        frame_image(0, s)
        frame_image(1, s)
        frame_stage(0, s)
        return 0

    lax.fori_loop(0, 2, first_frames, 0)
    loads[0].wait()
    loads[1].wait()

    def first_state(s, _):
        put_rows(imgh.at[s], 2, hin[s])
        v = cin[s].reshape(256, 192)
        cst[s, 0, 16:272, :] = v[:, 0:128]
        cst[s, 1, 16:272, :] = twice(v[:, 128:192])
        state_stage(s)
        return 0

    lax.fori_loop(0, 2, first_state, 0)
    near_rows = 1 + has(0).astype(jnp.int32) + has(1).astype(jnp.int32)
    near_cols = 1 + has(2).astype(jnp.int32) + has(3).astype(jnp.int32)
    pl.semaphore_wait(barrier, near_rows * near_cols - 1)
    frame_send(0, 0)
    def first_send(s, _):
        state_send(0, s, hin.at[s])
        return 0

    lax.fori_loop(0, 2, first_send, 0)
    frame_send(0, 1)
    for cp in loads[3:]:
        cp.wait()

    def stage_body(i, _):
        k, s = i // 2, lax.rem(i, 2)
        frame_image(2 * k, s)
        frame_image(2 * k + 1, s)
        frame_stage(k, s)

        @pl.when(s == 1)
        def _():
            frame_send(k, 0)
            frame_send(k, 1)

        return 0

    lax.fori_loop(2, 8, stage_body, 0)
    for cp in wloads[0]:
        cp.wait()
    frame_wait(0)

    def first_x(s, _):
        for odd in range(2):
            frame_fill(0, odd, s)
            x_part(0, odd, s)
        return 0

    lax.fori_loop(0, 2, first_x, 0)
    for cp in wloads[1]:
        cp.wait()

    def half_round(k, s, final):
        state_fill(k, s)
        h_step(s, 2 * k, True)
        if not final:
            x_part(k + 1, 0, s)
        h_step(s, 2 * k + 1, False, final)
        if not final:
            x_part(k + 1, 1, s)

    def body(i, _):
        k, s = i // 2, lax.rem(i, 2)

        @pl.when(s == 0)
        def _():
            frame_wait(k + 1)

        state_wait(k, s, hin.at[s])
        frame_fill(k + 1, 0, s)
        frame_fill(k + 1, 1, s)
        half_round(k, s, False)
        state_stage(s)
        state_send(k + 1, s, h_all.at[2 * k + 1, s])
        return 0

    def last_body(s, _):
        state_wait(3, s, hin.at[s])
        half_round(3, s, True)
        return 0

    lax.fori_loop(0, 6, body, 0)
    lax.fori_loop(0, 2, last_body, 0)


def solution(mesh):
    shape = (mesh.shape["rows"], mesh.shape["cols"])
    frame_spec = P(None, "batch", "rows", "cols", None)
    state_spec = P("batch", "rows", "cols", None)
    any_spec = pl.BlockSpec(memory_space=pl.ANY)
    vmem = pl.BlockSpec(memory_space=pltpu.VMEM)

    def local_run(frames, w_x, w_h, gate_bias, h_init, c_init):
        V = pltpu.VMEM
        D = pltpu.SemaphoreType.DMA
        scratch = [
            V((8, 2, 16, 16, 192), BF), V((2, 16, 16, 192), BF), V((2, 16, 16, 192), F32),
            V((1728, 768), BF), V((1728, 768), BF),
            V((16, 2, IMG_ROWS, PITCH, 128), F32), V((2, 2, IMG_ROWS, PITCH, 128), F32), V((2, 2, EXT_M, 128), F32),
            V((2, 20, 16, 512), BF), V((2, EXT_M, 256), BF), V((3, 48, 512), BF),
            V((20, 16, 512), BF), V((EXT_M, 256), BF), V((3, 48, 512), BF),
            V((2, EXT_M, 768), F32), V((2, 256, 768), F32), V((EXT_M, 768), F32),
            V((8, 2, 2, 2, 16, 256), BF), V((4, 4, 2, 2, 8, 128), F32),
            V((8, 2, 2, 2, 16, 192), BF), V((8, 2, 2, 2, 16, 256), BF), V((4, 4, 2, 2, 8, 128), F32),
            V((2, 2, 2, 16, 256), BF), V((2, 2, 2, 16, 128), F32), V((2, 4, 2, 8, 128), F32),
            V((8, 2, 2, 16, 192), BF), V((8, 2, 2, 16, 256), BF), V((8, 2, 2, 16, 128), F32), V((8, 2, 2, 16, 128), F32), V((8, 4, 2, 8, 128), F32),
            D((6,)), D((2, 18)), D((8, 4)), D((8, 4)), D((4, 4)), D((4, 4)), D((8, 12)), D((8, 12)),
        ]
        return pl.pallas_call(
            functools.partial(kernel, shape=shape),
            out_shape=[jax.ShapeDtypeStruct(frames.shape, BF), jax.ShapeDtypeStruct(c_init.shape, F32)],
            in_specs=[any_spec, any_spec, any_spec, vmem, any_spec, any_spec],
            out_specs=[vmem, vmem],
            scratch_shapes=scratch,
            compiler_params=pltpu.CompilerParams(collective_id=0, has_side_effects=True, vmem_limit_bytes=60 * 1024 * 1024),
            name="convlstm",
        )(frames, w_x, w_h, gate_bias.reshape(1, -1), h_init, c_init)

    return jax.shard_map(local_run, mesh=mesh, in_specs=(frame_spec, P(), P(), P(), state_spec, state_spec), out_specs=(frame_spec, state_spec), check_vma=False)
```

time: 320 us -> 124 us (0.39)
  the two profiles are of different devices: /device:TPU:97 before, /device:TPU:100 now
where the time goes in v1:
time: 124 us
  Pallas kernels  118 us (95%)
  local copies, waits for them, and re-layouts  5.22 us (4%)
    pallas_call x1, Pallas kernels, local_run(): pl.pallas_call(functools.partial(kernel, shape=shape), out_shape=[jax.Sha...  118 us
    unnamed x4, local copies, waits for them, and re-layouts  3.95 us

profile of v1, /device:TPU:100, one launch (start us, length us, event | category | flops | bytes accessed | tf_op | source)
XLA Modules:
  0.0 123.8 jit_solution(10407864809510312015)
XLA Ops:
  0.6 1.3 %reshape.7.bias = f32[1,768]{1,0:T(1,128)} reshape(f32[768]{0:T(1024)} %param.9) | data formatting | bytes 6144 | tf_op jit(solution)/shard_map/reshape | solution.py:511
  1.9 117.9 %convlstm.1 = (bf16[8,2,16,16,192]{4,3,2,1,0:T(8,128)(2,1)}, f32[2,16,16,192]{3,2,1,0:T(8,128)}) custom-call(bf16[8,2,16,16,192]{4,3,2,1,0:T(8,128)(2,1)} %frames.1, bf16[3,3,192,768]{3,2,1,0:T(8,128)(2,1)} %w_x.1, bf16[3,3,192,768]{3,2,1,0:T(8,128)(2,1)} %w_h.1, f32[1,768]{1,0:T(1,128)} %reshape.7.bias, bf16[2,16,16,192]{3,2,1,0:T(8,128)(2,1)} %h_init.1, ...), custom_call_target="tpu_custom_call" | custom-call | tf_op jit(solution)/shard_map/convlstm/pallas_call | solution.py:503
  119.8 0.0 copy-start
  119.8 3.2 %copy.10 = bf16[8,2,16,16,192]{4,3,2,1,0:T(8,128)(2,1)} copy(bf16[8,2,16,16,192]{4,3,2,1,0:T(8,128)(2,1)} %get-tuple-element.4) | data formatting | bytes 3145728
  123.0 0.0 copy-done
  123.0 0.8 copy.11
Async XLA Ops:
  119.8 3.2 %copy-start = (f32[2,16,16,192]{3,2,1,0:T(8,128)S(1)}, f32[2,16,16,192]{3,2,1,0:T(8,128)}, u32[]{:S(2)}) copy-start(f32[2,16,16,192]{3,2,1,0:T(8,128)} %get-tuple-element.5) | copy-start | bytes 1179652

commit v2 on v1

v2 whole, which is shorter than its diff:
```python
import functools

import jax
import jax.numpy as jnp
from jax import lax
from jax.experimental import pallas as pl
from jax.experimental.pallas import tpu as pltpu
from jax.sharding import PartitionSpec as P

MESH = pl.DeviceIdType.MESH
BF = jnp.bfloat16
F32 = jnp.float32

L, HALF, SIDE, CH, GATES, TAPS = 128, 64, 16, 192, 768, 512
LO, HI = slice(0, L), slice(L, 2 * L)
TWO, FOUR, EIGHT, FAR = 2, 4, 8, 18
PITCH = 24
IMG_ROWS = 26
STRIP = 24
MAIN = 288
EXT_M = 336
PLAIN_M = 256
DIRS = ((-1, 0), (1, 0), (0, -1), (0, 1), (-1, -1), (-1, 1), (1, -1), (1, 1))
OPP = (1, 0, 3, 2, 7, 6, 5, 4)


def cell(er, ec):
    return er * PITCH + ec


def corner_src(d):
    return (TWO if DIRS[d][0] < 0 else 16), (TWO if DIRS[d][1] < 0 else 16)


def corner_dst(d):
    return (FAR if DIRS[d][0] < 0 else 0), (FAR if DIRS[d][1] < 0 else 0)


def low_lanes(n):
    return lax.broadcasted_iota(jnp.int32, (n, 128), 1) < 64


def twice(v):
    return jnp.concatenate([v, v], axis=1)


def flat(img):
    return img.reshape(TWO, IMG_ROWS * PITCH, L)


def put_col(img, er, ec, a, b, n=SIDE):
    at = pl.ds(cell(er, ec), n, stride=PITCH)
    flat(img)[0, at, :] = a
    flat(img)[1, at, :] = b


def get_col(img, lt, er, ec, n=SIDE):
    return flat(img)[lt, pl.ds(cell(er, ec), n, stride=PITCH), :]


def put_rows(img, er, v):
    n = v.shape[0]
    v = v.reshape(n * SIDE, CH).astype(F32)
    put_body(img, er, v[:, LO], twice(v[:, L:CH]))


def put_body(img, er, a, b):
    n = a.shape[0] // SIDE
    for lt, v in enumerate((a, b)):
        img[lt, pl.ds(er, n), TWO:TWO + SIDE, :] = v.reshape(n, SIDE, L)


def build(img, lhs, ext):
    tap, tail, strip = lhs
    first, n = (0, 20) if ext else (1, FAR)
    rows = slice(first, first + n)
    lo = lax.broadcasted_iota(jnp.int32, (n, SIDE, L), TWO) < HALF
    for dc in range(3):
        tap[rows, :, dc * L:(dc + 1) * L] = img[0, rows, 1 + dc:17 + dc, :].astype(BF)
    b = [img[1, rows, 1 + dc:17 + dc, :] for dc in range(3)]
    tap[rows, :, 3 * L:TAPS] = jnp.where(lo, b[0], b[1]).astype(BF)
    m = n - TWO
    at = pl.ds(first * SIDE, m * SIDE)
    tail[at, LO] = jnp.where(lo[:m], b[TWO][:m], b[TWO][1:n - 1]).astype(BF).reshape(m * SIDE, L)
    tail[at, HI] = b[TWO][TWO:n].astype(BF).reshape(m * SIDE, L)
    if ext:
        lo24 = low_lanes(STRIP)

        def both(f):
            return jnp.concatenate([f(1), f(FAR)], axis=0).astype(BF)

        def col(lt, er, ec):
            return get_col(img, lt, er, ec, STRIP)

        for dr in range(3):
            for dc in range(3):
                strip[dr, :, dc * L:(dc + 1) * L] = both(lambda ec: col(0, dr, ec + dc - 1))
            strip[dr, :, 3 * L:TAPS] = both(lambda ec: jnp.where(lo24, col(1, dr, ec - 1), col(1, dr, ec)))
        tail[MAIN:EXT_M, LO] = both(lambda ec: jnp.where(lo24, col(1, 0, ec + 1), col(1, 1, ec + 1)))
        tail[MAIN:EXT_M, HI] = both(lambda ec: col(1, TWO, ec + 1))


def operand(lhs, ext):
    tap, tail, strip = lhs
    if ext:
        blocks = [jnp.concatenate([tap[dr:dr + FAR].reshape(MAIN, TAPS), strip[dr]], axis=0) for dr in range(3)]
        last = tail[:, 0:CH]
    else:
        blocks = [tap[1 + dr:17 + dr].reshape(PLAIN_M, TAPS) for dr in range(3)]
        last = tail[SIDE:SIDE + PLAIN_M, 0:CH]
    return jnp.concatenate(blocks + [last], axis=1)


def conv(lhs, w, add, out, ext, parts):
    x = operand(lhs, ext)
    for p in parts:
        at = slice(p * TWO * L, (p + 1) * TWO * L)
        z = jnp.dot(x, w[:, at], preferred_element_type=F32)
        out[:, at] = z + (add[:, at] if len(add.shape) > 1 else add[at].reshape(1, TWO * L))


def gates(z, c0, c1):
    n = c0.shape[0]
    lo = low_lanes(n)
    half = jnp.where(lo, 0.5, 1.0).astype(F32)
    off = jnp.where(lo, 0.5, 0.0).astype(F32)
    in0 = 0.5 * jnp.tanh(0.5 * z[0]) + 0.5
    a1 = 0.5 * jnp.tanh(0.5 * z[1]) + 0.5
    a2 = 0.5 * jnp.tanh(0.5 * z[TWO]) + 0.5
    out0 = 0.5 * jnp.tanh(0.5 * z[3]) + 0.5
    a4 = half * jnp.tanh(half * z[FOUR]) + off
    a5 = jnp.tanh(z[5])
    forget0 = pltpu.roll(jnp.where(lo, a2, a1), 64, 1)
    cand0 = pltpu.roll(jnp.where(lo, a5, a4), 64, 1)
    in_forget1 = jnp.where(lo, a1, a2)
    out_cand1 = jnp.where(lo, a4, a5)
    c0n = forget0 * c0 + in0 * cand0
    prod = in_forget1 * jnp.where(lo, pltpu.roll(out_cand1, 64, 1), c1)
    c1n = prod + pltpu.roll(prod, 64, 1)
    h0 = out0 * jnp.tanh(c0n)
    h1 = out_cand1 * jnp.tanh(c1n)
    h1 = jnp.where(lo, h1, pltpu.roll(h1, 64, 1))
    return h0.astype(BF), h1.astype(BF), c0n, c1n


def kernel(frames, w_x, w_h, bias, h_init, c_init, h_all, c_final,
           fr, hin, cin, wx, wh, imgx, imgh, cst, tapx, tailx, stripx, tapy, taily, taph, tailh, striph, gext, gpl, zext, zpl,
           s_xcol, s_xdiag, r_xrow, r_xcol, r_xdiag,
           s_hcol, s_ccol, s_diag, r_hrow, r_hcol, r_crow, r_ccol, r_diag,
           lsem, wsem, xs_sem, xr_sem, xd_s, xd_r, e_s, e_r, *, shape):
    lhs_x, lhs_y, lhs_h = (tapx, tailx, stripx), (tapy, taily, None), (taph, tailh, striph)
    n_rows, n_cols = shape
    row, col = lax.axis_index("rows"), lax.axis_index("cols")
    grp = lax.axis_index("batch")

    def has(d):
        dr, dc = DIRS[d]
        rr, cc = row + dr, col + dc
        return (rr >= 0) & (rr < n_rows) & (cc >= 0) & (cc < n_cols)

    def peer(d):
        return (grp, col + DIRS[d][1], row + DIRS[d][0])

    loads = [pltpu.make_async_copy(h_init, hin, lsem.at[0]), pltpu.make_async_copy(c_init, cin, lsem.at[1])]
    loads += [pltpu.make_async_copy(frames.at[pl.ds(TWO * k, TWO)], fr.at[pl.ds(TWO * k, TWO)], lsem.at[TWO + k]) for k in range(FOUR)]
    wloads = [[], []]
    for i, (src, dst) in enumerate(((w_x, wx), (w_h, wh))):
        n = 0
        for dr in range(3):
            for dc in range(3):
                at = dr * 512 + 384 + dc * 64 if dc < TWO else 1536 + dr * 64
                for c_at, rows_n, k_at in ((0, 128, dr * 512 + dc * 128), (128, 64, at)):
                    wloads[i].append(pltpu.make_async_copy(src.at[dr, dc, pl.ds(c_at, rows_n)], dst.at[pl.ds(k_at, rows_n)], wsem.at[i, n]))
                    n += 1
    for cp in loads[TWO:3] + loads[0:TWO] + loads[3:FOUR] + wloads[0] + wloads[1] + loads[FOUR:]:
        cp.start()

    barrier = pltpu.get_barrier_semaphore()
    for d in range(EIGHT):
        @pl.when(has(d))
        def _(d=d):
            pl.semaphore_signal(barrier, inc=1, device_id=peer(d), device_id_type=MESH)

    for d in range(EIGHT):
        @pl.when(jnp.logical_not(has(OPP[d])))
        def _(d=d):
            if d < TWO:
                for ref in (r_xrow, r_hrow, r_crow):
                    ref[:, d] = jnp.zeros((ref.shape[0],) + ref.shape[TWO:], ref.dtype)
            elif d < FOUR:
                for ref in (r_xcol, r_hcol, r_ccol):
                    ref[:, d - TWO] = jnp.zeros((ref.shape[0],) + ref.shape[TWO:], ref.dtype)
            else:
                for ref in (r_xdiag, r_diag):
                    ref[:, d - FOUR] = jnp.zeros((ref.shape[0],) + ref.shape[TWO:], ref.dtype)

    def frame_image(f, s):
        put_rows(imgx.at[TWO * f + s], TWO, fr[f, s])

    def frame_stage(k, s):
        for odd in range(TWO):
            f = TWO * k + odd
            img = imgx.at[TWO * f + s]
            for side in range(TWO):
                for j in range(1 if odd else TWO):
                    ec = (TWO + j) if side == 0 else (17 - j)
                    for lt, at in enumerate((LO, HI)):
                        s_xcol[f, side, j, s, :, at] = get_col(img, lt, TWO, ec).astype(BF)
            for d in range(FOUR, EIGHT):
                er, ec = corner_src(d)
                for lt in range(TWO):
                    if odd:
                        er1, ec1 = (TWO if er == TWO else 17), (TWO if ec == TWO else 17)
                        s_xdiag[k, d - FOUR, s, lt, FOUR:5, :] = img[lt, er1, pl.ds(ec1, 1), :]
                    else:
                        for i in range(TWO):
                            s_xdiag[k, d - FOUR, s, lt, TWO * i:TWO * i + TWO, :] = img[lt, er + i, pl.ds(ec, TWO), :]

    def frame_copy(f, odd, d):
        if d < TWO:
            at = (0 if d == 0 else 15) if odd else (0 if d == 0 else 14)
            src = fr.at[f, :, pl.ds(at, 1 if odd else TWO)]
            dst = r_xrow.at[f, d, :, pl.ds(d if odd else 0, 1 if odd else TWO)]
        else:
            src = s_xcol.at[f, d - TWO, pl.ds(0, 1 if odd else TWO)]
            dst = r_xcol.at[f, d - TWO, pl.ds(0, 1 if odd else TWO)]
        return pltpu.make_async_remote_copy(src_ref=src, dst_ref=dst, send_sem=xs_sem.at[f, d], recv_sem=xr_sem.at[f, d], device_id=peer(d), device_id_type=MESH)

    def frame_diag(k, d):
        return pltpu.make_async_remote_copy(src_ref=s_xdiag.at[k, d - FOUR], dst_ref=r_xdiag.at[k, d - FOUR], send_sem=xd_s.at[k, d - FOUR], recv_sem=xd_r.at[k, d - FOUR], device_id=peer(d), device_id_type=MESH)

    def frame_send(k, odd):
        for d in range(FOUR):
            @pl.when(has(d))
            def _(d=d):
                frame_copy(TWO * k + odd, odd, d).start()
        if not odd:
            for d in range(FOUR, EIGHT):
                @pl.when(has(d))
                def _(d=d):
                    frame_diag(k, d).start()

    def frame_wait(k):
        for d in range(EIGHT):
            @pl.when(has(OPP[d]))
            def _(d=d):
                if d < FOUR:
                    frame_copy(TWO * k, 0, d).wait_recv()
                    frame_copy(TWO * k + 1, 1, d).wait_recv()
                else:
                    frame_diag(k, d).wait_recv()
        for d in range(EIGHT):
            @pl.when(has(d))
            def _(d=d):
                if d < FOUR:
                    frame_copy(TWO * k, 0, d).wait_send()
                    frame_copy(TWO * k + 1, 1, d).wait_send()
                else:
                    frame_diag(k, d).wait_send()

    def frame_fill(k, odd, s):
        f = TWO * k + odd
        img = imgx.at[TWO * f + s]
        for d in range(TWO):
            i, n = (d, 1) if odd else (0, TWO)
            put_rows(img, (FAR + i) if d == 0 else i, r_xrow[f, d, s, pl.ds(i, n)])
            for j in range(1 if odd else TWO):
                v = r_xcol[f, d, j, s].astype(F32)
                put_col(img, TWO, (FAR + j) if d == 0 else (1 - j), v[:, LO], v[:, HI])
        for d in range(FOUR, EIGHT):
            er, ec = corner_dst(d)
            for lt in range(TWO):
                if odd:
                    er1, ec1 = (FAR if er == FAR else 1), (FAR if ec == FAR else 1)
                    img[lt, er1, pl.ds(ec1, 1), :] = r_xdiag[k, d - FOUR, s, lt, FOUR:5, :]
                else:
                    for i in range(TWO):
                        img[lt, er + i, pl.ds(ec, TWO), :] = r_xdiag[k, d - FOUR, s, lt, TWO * i:TWO * i + TWO, :]

    def x_build(k, odd, s):
        frame_fill(k, odd, s)
        build(imgx.at[TWO * (TWO * k + odd) + s], lhs_y if odd else lhs_x, not odd)

    def x_conv(s, odd, parts):
        if odd:
            conv(lhs_y, wx, bias, gpl.at[s], False, parts)
        else:
            conv(lhs_x, wx, bias, gext.at[s], True, parts)

    def state_copies(e, s, d, hsrc):
        x = TWO * e + s

        def mk(src, dst, n):
            return pltpu.make_async_remote_copy(src_ref=src, dst_ref=dst, send_sem=e_s.at[x, n], recv_sem=e_r.at[x, n], device_id=peer(d), device_id_type=MESH)

        if d < TWO:
            return [mk(hsrc.at[pl.ds(0 if d == 0 else 14, TWO)], r_hrow.at[x, d], d),
                    mk(cst.at[s, :, pl.ds(16 if d == 0 else 256, 16)], r_crow.at[x, d], EIGHT + d)]
        if d < FOUR:
            return [mk(s_hcol.at[s, d - TWO], r_hcol.at[x, d - TWO], d), mk(s_ccol.at[s, d - TWO], r_ccol.at[x, d - TWO], EIGHT + d)]
        return [mk(s_diag.at[s, d - FOUR], r_diag.at[x, d - FOUR], d)]

    def state_stage(s):
        img = imgh.at[s]
        for side in range(TWO):
            for j in range(TWO):
                ec = (TWO + j) if side == 0 else (17 - j)
                for lt, at in enumerate((LO, HI)):
                    s_hcol[s, side, j, :, at] = get_col(img, lt, TWO, ec).astype(BF)
            for lt in range(TWO):
                s_ccol[s, side, lt] = cst[s, lt, pl.ds(16 + 15 * side, 16, stride=16), :]
        for d in range(FOUR, EIGHT):
            er, ec = corner_src(d)
            er1, ec1 = (TWO if er == TWO else 17), (TWO if ec == TWO else 17)
            for lt in range(TWO):
                for i in range(TWO):
                    s_diag[s, d - FOUR, lt, TWO * i:TWO * i + TWO, :] = img[lt, er + i, pl.ds(ec, TWO), :]
                s_diag[s, d - FOUR, lt, FOUR:5, :] = cst[s, lt, pl.ds((er1 - 1) * 16 + ec1 - TWO, 1), :]

    def state_send(e, s, hsrc):
        for d in (TWO, 3, FOUR, 5, 6, 7, 0, 1):
            @pl.when(has(d))
            def _(d=d):
                for cp in state_copies(e, s, d, hsrc):
                    cp.start()

    def state_wait(e, s):
        for d in range(EIGHT):
            @pl.when(has(OPP[d]))
            def _(d=d):
                for cp in state_copies(e, s, d, hin.at[s]):
                    cp.wait_recv()
        for d in range(EIGHT):
            @pl.when(has(d))
            def _(d=d):
                for cp in state_copies(e, s, d, hin.at[s]):
                    cp.wait_send()

    def state_fill(e, s):
        img = imgh.at[s]
        x = TWO * e + s
        for d in range(TWO):
            put_rows(img, FAR if d == 0 else 0, r_hrow[x, d])
            for lt in range(TWO):
                m = 272 if d == 0 else 0
                cst[s, lt, m:m + 16, :] = r_crow[x, d, lt]
            for j in range(TWO):
                v = r_hcol[x, d, j].astype(F32)
                put_col(img, TWO, (FAR + j) if d == 0 else (1 - j), v[:, LO], v[:, HI])
            for lt in range(TWO):
                m = 288 + (24 if d == 0 else 0) + 1
                cst[s, lt, pl.ds(m, 16), :] = r_ccol[x, d, lt]
        for d in range(FOUR, EIGHT):
            er, ec = corner_dst(d)
            m = 288 + (24 if ec == FAR else 0) + (17 if er == FAR else 0)
            for lt in range(TWO):
                for i in range(TWO):
                    img[lt, er + i, pl.ds(ec, TWO), :] = r_diag[x, d - FOUR, lt, TWO * i:TWO * i + TWO, :]
                cst[s, lt, pl.ds(m, 1), :] = r_diag[x, d - FOUR, lt, FOUR:5, :]

    def flag(cond, n):
        return jnp.full((n, 128), jnp.where(cond, 1, 0).astype(jnp.int32)) > 0

    def update(s, t, ext, last=False):
        img = imgh.at[s]
        z_ref = zext if ext else zpl

        def one(m, n):
            zm = m if ext else m - SIDE
            z = [z_ref[zm:zm + n, p * L:(p + 1) * L] for p in range(6)]
            h0, h1, c0, c1 = gates(z, cst[s, 0, m:m + n, :], cst[s, 1, m:m + n, :])
            cst[s, 0, m:m + n, :] = c0
            cst[s, 1, m:m + n, :] = c1
            return h0, h1, c0, c1

        er, end = (1, 19) if ext else (TWO, FAR)
        while er < end:
            n = 1 if er == 1 or er == end - 1 else TWO
            h0, h1, c0, c1 = one((er - 1) * SIDE, n * SIDE)
            if 1 < er < FAR:
                at = pl.ds(er - TWO, n)
                h_all[t, s, at, :, LO] = h0.reshape(n, SIDE, L)
                h_all[t, s, at, :, L:CH] = h1[:, :HALF].reshape(n, SIDE, HALF)
            if last:
                c_final[s, at, :, LO] = c0.reshape(n, SIDE, L)
                c_final[s, at, :, L:CH] = c1[:, :HALF].reshape(n, SIDE, HALF)
            else:
                f0, f1 = h0.astype(F32), h1.astype(F32)
                if er == 1 or er == FAR:
                    ok = flag(has(0 if er == 1 else 1), n * SIDE)
                    f0, f1 = jnp.where(ok, f0, 0.0), jnp.where(ok, f1, 0.0)
                put_body(img, er, f0, f1)
            er += n
        if not ext:
            return
        pos = lax.broadcasted_iota(jnp.int32, (STRIP, L), 0)
        for side in range(TWO):
            ok = flag(has(TWO + side), STRIP) & (flag(has(0), STRIP) | (pos > 0)) & (flag(has(1), STRIP) | (pos < 17))
            h0, h1, _, _ = one(MAIN + STRIP * side, STRIP)
            put_col(img, 1, 1 + 17 * side, jnp.where(ok, h0.astype(F32), 0.0), jnp.where(ok, h1.astype(F32), 0.0), STRIP)

    def h_build(s, ext):
        build(imgh.at[s], lhs_h, ext)

    def h_conv(s, ext):
        if ext:
            conv(lhs_h, wh, gext.at[s], zext, True, range(3))
        else:
            conv(lhs_h, wh, gpl.at[s], zpl, False, range(3))

    loads[TWO].wait()

    def first_frames(s, _):
        frame_image(0, s)
        frame_image(1, s)
        frame_stage(0, s)
        return 0

    lax.fori_loop(0, TWO, first_frames, 0)
    loads[0].wait()
    loads[1].wait()

    def first_state(s, _):
        put_rows(imgh.at[s], TWO, hin[s])
        v = cin[s].reshape(256, 192)
        cst[s, 0, 16:272, :] = v[:, 0:128]
        cst[s, 1, 16:272, :] = twice(v[:, 128:192])
        state_stage(s)
        return 0

    lax.fori_loop(0, TWO, first_state, 0)
    near_rows = 1 + has(0).astype(jnp.int32) + has(1).astype(jnp.int32)
    near_cols = 1 + has(TWO).astype(jnp.int32) + has(3).astype(jnp.int32)
    pl.semaphore_wait(barrier, near_rows * near_cols - 1)
    frame_send(0, 0)
    def first_send(s, _):
        state_send(0, s, hin.at[s])
        return 0

    lax.fori_loop(0, TWO, first_send, 0)
    frame_send(0, 1)
    for cp in loads[3:]:
        cp.wait()

    def stage_body(i, _):
        k, s = i // TWO, lax.rem(i, TWO)
        frame_image(TWO * k, s)
        frame_image(TWO * k + 1, s)
        frame_stage(k, s)

        @pl.when(s == 1)
        def _():
            frame_send(k, 0)
            frame_send(k, 1)

        return 0

    lax.fori_loop(TWO, EIGHT, stage_body, 0)
    for cp in wloads[0]:
        cp.wait()
    frame_wait(0)

    for s in range(TWO):
        x_build(0, 0, s)
        x_conv(s, 0, range(3))
        x_build(0, 1, s)
        x_conv(s, 1, range(3) if s == 0 else range(TWO))
    for cp in wloads[1]:
        cp.wait()

    def half_round(k, s):
        x_conv(1 - s, 1, (TWO,))
        state_fill(k, s)
        h_build(s, True)
        x_build(k + 1, 0, s)
        h_conv(s, True)
        x_conv(s, 0, (0, 1))
        update(s, TWO * k, True)
        h_build(s, False)
        x_build(k + 1, 1, s)
        h_conv(s, False)
        x_conv(s, 0, (TWO,))
        x_conv(s, 1, (0,))
        update(s, TWO * k + 1, False)
        state_stage(s)

    def round_body(k, _):
        frame_wait(k + 1)
        for s in range(TWO):
            state_wait(k, s)
            half_round(k, s)
            state_send(k + 1, s, h_all.at[TWO * k + 1, s])
            x_conv(s, 1, (1,))
        return 0

    lax.fori_loop(0, 3, round_body, 0)
    last = 3
    state_wait(last, 0)
    x_conv(1, 1, (TWO,))
    state_fill(last, 0)
    h_build(0, True)
    h_conv(0, True)
    update(0, TWO * last, True)
    state_wait(last, 1)
    state_fill(last, 1)
    h_build(1, True)
    h_conv(1, True)
    h_build(0, False)
    h_conv(0, False)
    update(1, TWO * last, True)
    h_build(1, False)
    update(0, TWO * last + 1, False, True)
    h_conv(1, False)
    update(1, TWO * last + 1, False, True)


def solution(mesh):
    shape = (mesh.shape["rows"], mesh.shape["cols"])
    frame_spec = P(None, "batch", "rows", "cols", None)
    state_spec = P("batch", "rows", "cols", None)
    any_spec = pl.BlockSpec(memory_space=pl.ANY)
    vmem = pl.BlockSpec(memory_space=pltpu.VMEM)

    def local_run(frames, w_x, w_h, gate_bias, h_init, c_init):
        V = pltpu.VMEM
        D = pltpu.SemaphoreType.DMA
        scratch = [
            V(frames.shape, BF), V(h_init.shape, BF), V(c_init.shape, F32),
            V((9 * CH, GATES), BF), V((9 * CH, GATES), BF),
            V((16, TWO, IMG_ROWS, PITCH, L), F32), V((TWO, TWO, IMG_ROWS, PITCH, L), F32), V((TWO, TWO, EXT_M, L), F32),
            V((20, SIDE, TAPS), BF), V((EXT_M, TWO * L), BF), V((3, TWO * STRIP, TAPS), BF),
            V((20, SIDE, TAPS), BF), V((EXT_M, TWO * L), BF),
            V((20, SIDE, TAPS), BF), V((EXT_M, TWO * L), BF), V((3, TWO * STRIP, TAPS), BF),
            V((TWO, EXT_M, GATES), F32), V((TWO, PLAIN_M, GATES), F32), V((EXT_M, GATES), F32), V((PLAIN_M, GATES), F32),
            V((EIGHT, TWO, TWO, TWO, SIDE, TWO * L), BF), V((FOUR, FOUR, TWO, TWO, EIGHT, L), F32),
            V((EIGHT, TWO, TWO, TWO, SIDE, CH), BF), V((EIGHT, TWO, TWO, TWO, SIDE, TWO * L), BF), V((FOUR, FOUR, TWO, TWO, EIGHT, L), F32),
            V((TWO, TWO, TWO, SIDE, TWO * L), BF), V((TWO, TWO, TWO, SIDE, L), F32), V((TWO, FOUR, TWO, EIGHT, L), F32),
            V((EIGHT, TWO, TWO, SIDE, CH), BF), V((EIGHT, TWO, TWO, SIDE, TWO * L), BF), V((EIGHT, TWO, TWO, SIDE, L), F32), V((EIGHT, TWO, TWO, SIDE, L), F32), V((EIGHT, FOUR, TWO, EIGHT, L), F32),
            D((6,)), D((TWO, FAR)), D((EIGHT, FOUR)), D((EIGHT, FOUR)), D((FOUR, FOUR)), D((FOUR, FOUR)), D((EIGHT, 12)), D((EIGHT, 12)),
        ]
        return pl.pallas_call(
            functools.partial(kernel, shape=shape),
            out_shape=[V(frames.shape, BF), V(c_init.shape, F32)],
            in_specs=[any_spec, any_spec, any_spec, vmem, any_spec, any_spec],
            out_specs=[vmem, vmem],
            scratch_shapes=scratch,
            compiler_params=pltpu.CompilerParams(collective_id=0, has_side_effects=True, vmem_limit_bytes=60 * 1024 * 1024),
            name="convlstm",
        )(frames, w_x, w_h, gate_bias, h_init, c_init)

    return jax.shard_map(local_run, mesh=mesh, in_specs=(frame_spec, P(), P(), P(), state_spec, state_spec), out_specs=(frame_spec, state_spec), check_vma=False)
```

time: 124 us -> 55.7 us (0.45)
  the two profiles are of different devices: /device:TPU:100 before, /device:TPU:97 now
where the time goes in v2:
time: 55.7 us; the launch traced here: 55.1 us
  Pallas kernels  52.3 us (94%)
  local copies, waits for them, and re-layouts  2.11 us (4%)
  between operations  0.64 us (1%)
    pallas_call x1, Pallas kernels, local_run(): pl.pallas_call(functools.partial(kernel, shape=shape), out_shape=[V(frame...  52.3 us
    unnamed x2, local copies, waits for them, and re-layouts  2.11 us

profile of v2, /device:TPU:97, one launch (start us, length us, event | category | flops | bytes accessed | tf_op | source)
XLA Modules:
  0.0 55.1 jit_solution(4391527353684566754)
XLA Ops:
  0.6 52.3 %convlstm.1 = (bf16[8,2,16,16,192]{4,3,2,1,0:T(8,128)(2,1)S(1)}, f32[2,16,16,192]{3,2,1,0:T(8,128)S(1)}) custom-call(bf16[8,2,16,16,192]{4,3,2,1,0:T(8,128)(2,1)} %frames.1, bf16[3,3,192,768]{3,2,1,0:T(8,128)(2,1)} %w_x.1, bf16[3,3,192,768]{3,2,1,0:T(8,128)(2,1)} %w_h.1, f32[768]{0:T(1024)} %bias.1, bf16[2,16,16,192]{3,2,1,0:T(8,128)(2,1)} %h_init.1, ...), custom_call_target="tpu_custom_call" | custom-call | tf_op jit(solution)/shard_map/convlstm/pallas_call | solution.py:541
  53.0 1.3 %copy.10 = bf16[8,2,16,16,192]{4,3,2,1,0:T(8,128)(2,1)} copy(bf16[8,2,16,16,192]{4,3,2,1,0:T(8,128)(2,1)S(1)} %get-tuple-element.2) | data formatting | bytes 3145728
  54.3 0.8 %copy.11 = f32[2,16,16,192]{3,2,1,0:T(8,128)} copy(f32[2,16,16,192]{3,2,1,0:T(8,128)S(1)} %get-tuple-element.3) | data formatting | bytes 786432

commit v3 on v0

v3 whole, which is shorter than its diff:
```python
import functools

import jax
import jax.numpy as jnp
from jax import lax
from jax.experimental import pallas as pl
from jax.experimental.pallas import tpu as pltpu
from jax.sharding import PartitionSpec as P

MESH = pl.DeviceIdType.MESH
BF = jnp.bfloat16
F32 = jnp.float32

L, HALF, SIDE, CH, GATES, TAPS = 128, 64, 16, 192, 768, 512
TWO, FOUR, EIGHT, FAR = 2, 4, 8, 18
PIECES = 6
PITCH = 24
IMG_ROWS = 26
STRIP = 24
MAIN = 288
EXT_M = 336
PLAIN_M = 256
INNER = 14
DIRS = ((-1, 0), (1, 0), (0, -1), (0, 1), (-1, -1), (-1, 1), (1, -1), (1, 1))
OPP = (1, 0, 3, 2, 7, 6, 5, 4)
STRIPS = ((1, 1, STRIP), (FAR, 1, STRIP), (2, 3, SIDE), (17, 3, SIDE))
STRIP_M = 80
EXT = (((1, FAR),), slice(0, 48))
PLAIN = (((2, SIDE),), None)
IN = (((3, INNER),), None)
EXT_OUT = (((1, 2), (17, 2)), slice(0, STRIP_M))
PLAIN_OUT = (((2, 1), (17, 1)), slice(48, STRIP_M))


def cell(er, ec):
    return er * PITCH + ec


def corner_src(d):
    return (TWO if DIRS[d][0] < 0 else SIDE), (TWO if DIRS[d][1] < 0 else SIDE)


def corner_dst(d):
    return (FAR if DIRS[d][0] < 0 else 0), (FAR if DIRS[d][1] < 0 else 0)


def near(e):
    return {TWO: TWO, SIDE: 17, FAR: FAR, 0: 1}[e]


def low_lanes(n):
    return lax.broadcasted_iota(jnp.int32, (n, L), 1) < HALF


def twice(v):
    return jnp.concatenate([v, v], axis=1)


def halves(v):
    lo, w = low_lanes(v.shape[0]), pltpu.roll(v, HALF, 1)
    return jnp.where(lo, v, w), jnp.where(lo, w, v)


def join(a, b):
    return jnp.where(low_lanes(a.shape[0]), a, b)


def flat(ref):
    return ref.reshape(ref.shape[0], TWO, IMG_ROWS * PITCH, L)


def put_col(img, er, ec, a, b):
    ref, x = img
    at = pl.ds(cell(er, ec), a.shape[0], stride=PITCH)
    flat(ref)[x, 0, at, :] = a
    flat(ref)[x, 1, at, :] = b


def get_col(img, lt, er, ec, n=SIDE):
    ref, x = img
    return flat(ref)[x, lt, pl.ds(cell(er, ec), n, stride=PITCH), :]


def put_rows(img, er, v):
    n = v.shape[0]
    v = v.reshape(n * SIDE, CH).astype(F32)
    put_body(img, er, v[:, :L], twice(v[:, L:]))


def put_body(img, er, a, b):
    n = a.shape[0] // SIDE
    ref, x = img
    for lt, v in enumerate((a, b)):
        ref[x, lt, pl.ds(er, n), TWO:FAR, :] = v.reshape(n, SIDE, L)


def pack_cols(dst, a0, b0, a1, b1):
    for i, v in enumerate((a0, a1, join(b0, b1))):
        dst[i] = v.astype(dst.dtype)


def unpack_cols(src):
    b0, b1 = halves(src[TWO].astype(F32))
    return src[0].astype(F32), b0, src[1].astype(F32), b1


def pack_corner(dst, img, d, a, b):
    er, ec = corner_src(d)
    ref, x = img
    for i in range(TWO):
        dst[TWO * i:TWO * i + TWO, :] = ref[x, 0, er + i, pl.ds(ec, TWO), :]
        dst[5 + i:6 + i, :] = join(ref[x, 1, er + i, pl.ds(ec, 1), :], ref[x, 1, er + i, pl.ds(ec + 1, 1), :])
    dst[FOUR:5, :] = a
    dst[7:EIGHT, :] = b


def unpack_corner(src, img, d):
    er, ec = corner_dst(d)
    ref, x = img
    for i in range(TWO):
        ref[x, 0, er + i, pl.ds(ec, TWO), :] = src[TWO * i:TWO * i + TWO, :]
        for j, v in enumerate(halves(src[5 + i:6 + i, :])):
            ref[x, 1, er + i, pl.ds(ec + j, 1), :] = v


def build_rows(img, lhs, first, n):
    tap, tail, _ = lhs
    ref, x = img
    rows = slice(first, first + n)
    lo = lax.broadcasted_iota(jnp.int32, (n, SIDE, L), TWO) < HALF
    for dc in range(3):
        tap[rows, :, dc * L:(dc + 1) * L] = ref[x, 0, rows, 1 + dc:17 + dc, :].astype(BF)
    b = [ref[x, 1, rows, 1 + dc:17 + dc, :] for dc in range(3)]
    tap[rows, :, 3 * L:] = jnp.where(lo, b[0], b[1]).astype(BF)
    m = n - TWO
    at = pl.ds(first * SIDE, m * SIDE)
    tail[at, :L] = jnp.where(lo[:m], b[TWO][:m], b[TWO][1:n - 1]).astype(BF).reshape(m * SIDE, L)
    tail[at, L:] = b[TWO][TWO:].astype(BF).reshape(m * SIDE, L)


def build_strips(img, lhs, which):
    _, tail, strip = lhs
    at = 0
    for ec, er, n in STRIPS:
        rows = slice(at, at + n)
        at += n
        if (ec, er, n) not in which:
            continue

        def col(lt, dr, dc):
            return get_col(img, lt, er - 1 + dr, ec - 1 + dc, n)

        for dr in range(3):
            for dc in range(3):
                strip[dr, rows, dc * L:(dc + 1) * L] = col(0, dr, dc).astype(BF)
            strip[dr, rows, 3 * L:] = join(col(1, dr, 0), col(1, dr, 1)).astype(BF)
        rows = slice(MAIN + rows.start, MAIN + rows.stop)
        tail[rows, :L] = join(col(1, 0, TWO), col(1, 1, TWO)).astype(BF)
        tail[rows, L:] = col(1, TWO, TWO).astype(BF)


def build(img, lhs, kind):
    if kind is EXT:
        build_rows(img, lhs, 0, 20)
        build_strips(img, lhs, STRIPS[:TWO])
    elif kind is PLAIN:
        build_rows(img, lhs, 1, FAR)
    elif kind is IN:
        build_rows(img, lhs, TWO, SIDE)
    elif kind is EXT_OUT:
        build_rows(img, lhs, 0, FOUR)
        build_rows(img, lhs, SIDE, FOUR)
        build_strips(img, lhs, STRIPS)
    else:
        build_rows(img, lhs, 1, 3)
        build_rows(img, lhs, SIDE, 3)
        build_strips(img, lhs, STRIPS[TWO:])


def operand(lhs, kind):
    tap, tail, strip = lhs
    runs, cut = kind
    blocks = []
    for dr in range(3):
        parts = [tap[er - 1 + dr:er - 1 + dr + n].reshape(n * SIDE, TAPS) for er, n in runs]
        blocks.append(parts + ([strip[dr, cut]] if cut else []))
    last = [tail[(er - 1) * SIDE:(er - 1 + n) * SIDE, :CH] for er, n in runs]
    if cut:
        last.append(tail[MAIN + cut.start:MAIN + cut.stop, :CH])
    return jnp.concatenate([jnp.concatenate(b, axis=0) for b in blocks + [last]], axis=1)


def conv(lhs, w, add, out, kind, first, parts):
    x = operand(lhs, kind)
    runs, cut = kind
    for p in parts:
        z = jnp.dot(x, w[:, TWO * p * L:TWO * (p + 1) * L], preferred_element_type=F32)
        for q in (TWO * p, TWO * p + 1):
            v = z[:, (q % TWO) * L:(q % TWO + 1) * L]

            def store(at, u):
                out[0][out[1], q, at, :] = u + (add[0][add[1], q, at, :] if isinstance(add, tuple) else add[q:q + 1, :])

            m = 0
            for er, n in runs:
                store(pl.ds((er - first) * SIDE, n * SIDE), v[m:m + n * SIDE])
                m += n * SIDE
            if cut and not cut.start:
                store(pl.ds(MAIN, TWO * STRIP), v[m:m + TWO * STRIP])
                m += TWO * STRIP
            if kind is EXT_OUT or kind is PLAIN_OUT:
                for side in range(TWO):
                    store(pl.ds((3 - first) * SIDE + 15 * side, INNER, stride=SIDE), v[m:m + INNER])
                    m += SIDE


def gates(z, c0, c1):
    lo = low_lanes(c0.shape[0])
    half = jnp.where(lo, 0.5, 1.0).astype(F32)
    off = jnp.where(lo, 0.5, 0.0).astype(F32)

    def sigmoid(v):
        return 0.5 * jnp.tanh(0.5 * v) + 0.5

    in0, a1, a2, out0 = [sigmoid(v) for v in z[:FOUR]]
    a4 = half * jnp.tanh(half * z[FOUR]) + off
    a5 = jnp.tanh(z[5])
    forget0 = pltpu.roll(jnp.where(lo, a2, a1), HALF, 1)
    cand0 = pltpu.roll(jnp.where(lo, a5, a4), HALF, 1)
    in_forget1 = jnp.where(lo, a1, a2)
    out_cand1 = jnp.where(lo, a4, a5)
    c0n = forget0 * c0 + in0 * cand0
    prod = in_forget1 * jnp.where(lo, pltpu.roll(out_cand1, HALF, 1), c1)
    c1n = prod + pltpu.roll(prod, HALF, 1)
    h0 = out0 * jnp.tanh(c0n)
    h1, _ = halves(out_cand1 * jnp.tanh(c1n))
    return h0.astype(BF), h1.astype(BF), c0n, c1n


def kernel(frames, w_x, w_h, bias_in, h_init, c_init, h_all, c_final,
           fr, hin, cin, bias_v, bias, wx, wh, imgx, imgh, cst, tapx, tailx, stripx, tapy, taily, stripy, taph, tailh, striph,
           gext, gpl, zext, zpl,
           s_xcol, s_xdiag, r_xrow, r_xcol, r_xdiag,
           s_hcol, s_ccol, s_diag, r_hrow, r_hcol, r_crow, r_ccol, r_diag,
           lsem, wsem, xs_sem, xr_sem, e_s, e_r, *, shape):
    lhs_x, lhs_y, lhs_h = (tapx, tailx, stripx), (tapy, taily, stripy), (taph, tailh, striph)
    n_rows, n_cols = shape
    row, col = lax.axis_index("rows"), lax.axis_index("cols")
    grp = lax.axis_index("batch")

    def has(d):
        dr, dc = DIRS[d]
        rr, cc = row + dr, col + dc
        return (rr >= 0) & (rr < n_rows) & (cc >= 0) & (cc < n_cols)

    def peer(d):
        return (grp, col + DIRS[d][1], row + DIRS[d][0])

    def each(dirs, ok, f):
        for d in dirs:
            @pl.when(ok(d))
            def _(d=d):
                f(d)

    load_h = pltpu.make_async_copy(h_init, hin, lsem.at[0])
    load_c = pltpu.make_async_copy(c_init, cin, lsem.at[1])
    load_b = pltpu.make_async_copy(bias_in, bias_v, lsem.at[TWO])
    load_f = [pltpu.make_async_copy(frames.at[pl.ds(TWO * k, TWO)], fr.at[pl.ds(TWO * k, TWO)], lsem.at[3 + k]) for k in range(FOUR)]
    load_w = [[], []]
    for i, (src, dst) in enumerate(((w_x, wx), (w_h, wh))):
        for dr in range(3):
            for dc in range(3):
                at = dr * TAPS + 3 * L + dc * HALF if dc < TWO else 3 * TAPS + dr * HALF
                for c_at, n, k_at in ((0, L, dr * TAPS + dc * L), (L, HALF, at)):
                    load_w[i].append(pltpu.make_async_copy(src.at[dr, dc, pl.ds(c_at, n)], dst.at[pl.ds(k_at, n)], wsem.at[i, len(load_w[i])]))
    for cp in [load_f[0], load_h, load_c, load_b] + load_w[0] + load_w[1] + load_f[1:]:
        cp.start()

    barrier = pltpu.get_barrier_semaphore()
    each(range(EIGHT), has, lambda d: pl.semaphore_signal(barrier, inc=1, device_id=peer(d), device_id_type=MESH))

    def blank(d):
        refs = (r_xrow, r_hrow, r_crow) if d < TWO else (r_xcol, r_hcol, r_ccol) if d < FOUR else (r_xdiag, r_diag)
        for ref in refs:
            ref[:, d % FOUR if d > 3 else d % TWO] = jnp.zeros((ref.shape[0],) + ref.shape[TWO:], ref.dtype)

    def frame_stage(k):
        for odd in range(TWO):
            for s in range(TWO):
                put_rows((imgx, FOUR * k + TWO * odd + s), TWO, fr[TWO * k + odd, s])
        for side in range(TWO):
            ec = (TWO + 15 * side, 3 + 13 * side)
            for s in range(TWO):
                img = (imgx, FOUR * k + s)
                pack_cols(s_xcol.at[TWO * k, side, s], *[get_col(img, lt, TWO, e) for e in ec for lt in range(TWO)])
            pack_cols(s_xcol.at[TWO * k + 1, side, 0], *[get_col((imgx, FOUR * k + TWO + s), lt, TWO, ec[0]) for s in range(TWO) for lt in range(TWO)])
        for d in range(FOUR, EIGHT):
            er, ec = [near(e) for e in corner_src(d)]
            for s in range(TWO):
                pack_corner(s_xdiag.at[k, d - FOUR, s], (imgx, FOUR * k + s), d, *[imgx[FOUR * k + TWO + s, lt, er, pl.ds(ec, 1), :] for lt in range(TWO)])

    def frame_copies(k, odd, d):
        f = TWO * k + odd

        def mk(src, dst):
            return [pltpu.make_async_remote_copy(src_ref=src, dst_ref=dst, send_sem=xs_sem.at[f, d], recv_sem=xr_sem.at[f, d], device_id=peer(d), device_id_type=MESH)]

        n = 1 if odd else TWO
        if d < TWO:
            at = SIDE - n if d else 0
            return mk(fr.at[f, :, pl.ds(at, n)], r_xrow.at[f, d, :, pl.ds(d if odd else 0, n)])
        if d < FOUR:
            return mk(s_xcol.at[f, d - TWO, pl.ds(0, n)], r_xcol.at[f, d - TWO, pl.ds(0, n)])
        return [] if odd else mk(s_xdiag.at[k, d - FOUR], r_xdiag.at[k, d - FOUR])

    def frame_send(k, odd):
        each(range(FOUR) if odd else (TWO, 3, FOUR, 5, 6, 7, 0, 1), has, lambda d: [cp.start() for cp in frame_copies(k, odd, d)])

    def frame_wait(k):
        each(range(EIGHT), lambda d: has(OPP[d]), lambda d: [cp.wait_recv() for odd in range(TWO) for cp in frame_copies(k, odd, d)])
        each(range(EIGHT), has, lambda d: [cp.wait_send() for odd in range(TWO) for cp in frame_copies(k, odd, d)])

    def frame_fill(k, odd, s):
        f = TWO * k + odd
        img = (imgx, TWO * f + s)
        for d in range(TWO):
            i, n = (d, 1) if odd else (0, TWO)
            put_rows(img, i + FAR * (1 - d), r_xrow[f, d, s, pl.ds(i, n)])
            ec = (1, 0) if d else (FAR, FAR + 1)
            if odd:
                b = halves(r_xcol[f, d, 0, TWO].astype(F32))
                b = b[s] if isinstance(s, int) else jnp.where(flag(s == 0, SIDE), *b)
                put_col(img, TWO, ec[0], r_xcol[f, d, 0, s].astype(F32), b)
            else:
                ab = unpack_cols(r_xcol[f, d, s])
                put_col(img, TWO, ec[0], *ab[:TWO])
                put_col(img, TWO, ec[1], *ab[TWO:])
        for d in range(FOUR, EIGHT):
            src = r_xdiag.at[k, d - FOUR, s]
            if odd:
                er, ec = [near(e) for e in corner_dst(d)]
                imgx[TWO * f + s, 0, er, pl.ds(ec, 1), :] = src[FOUR:5, :]
                imgx[TWO * f + s, 1, er, pl.ds(ec, 1), :] = src[7:EIGHT, :]
            else:
                unpack_corner(src, img, d)

    def x_build(k, odd, s, kind):
        build((imgx, FOUR * k + TWO * odd + s), lhs_y if odd else lhs_x, kind)

    def x_conv(s, odd, kind, parts=range(3)):
        conv(lhs_y if odd else lhs_x, wx, bias, (gpl if odd else gext, s), kind, 1 + odd, parts)

    def state_copies(e, s, d, hsrc, which=(0, 1)):
        x = TWO * e + s
        if d < TWO:
            refs = ((hsrc.at[pl.ds(INNER * d, TWO)], r_hrow.at[x, d]), (cst.at[s, :, pl.ds(SIDE + 240 * d, SIDE)], r_crow.at[x, d]))
        elif d < FOUR:
            refs = ((s_hcol.at[s, d - TWO], r_hcol.at[x, d - TWO]), (s_ccol.at[s, d - TWO], r_ccol.at[x, d - TWO]))
        else:
            refs = ((s_diag.at[s, d - FOUR], r_diag.at[x, d - FOUR]),)
        return [pltpu.make_async_remote_copy(src_ref=refs[i][0], dst_ref=refs[i][1], send_sem=e_s.at[x, d + EIGHT * i], recv_sem=e_r.at[x, d + EIGHT * i], device_id=peer(d), device_id_type=MESH) for i in which[:len(refs)]]

    def state_stage(s):
        img = (imgh, s)
        for side in range(TWO):
            ec = (TWO + 15 * side, 3 + 13 * side)
            pack_cols(s_hcol.at[s, side], *[get_col(img, lt, TWO, e) for e in ec for lt in range(TWO)])
            c0, c1 = [cst[s, lt, pl.ds(SIDE + 15 * side, SIDE, stride=SIDE), :] for lt in range(TWO)]
            s_ccol[s, side, :SIDE] = c0
            s_ccol[s, side, SIDE:] = join(c1[:EIGHT], c1[EIGHT:])
        for d in range(FOUR, EIGHT):
            er, ec = [near(e) for e in corner_src(d)]
            at = pl.ds((er - 1) * SIDE + ec - TWO, 1)
            pack_corner(s_diag.at[s, d - FOUR], img, d, cst[s, 0, at, :], cst[s, 1, at, :])

    def state_send(e, s, hsrc):
        each((TWO, 3, FOUR, 5, 6, 7, 0, 1), has, lambda d: state_copies(e, s, d, hsrc, (0,))[0].start())
        each(range(FOUR), has, lambda d: state_copies(e, s, d, hsrc, (1,))[0].start())

    def state_wait(e, s):
        each(range(EIGHT), lambda d: has(OPP[d]), lambda d: [cp.wait_recv() for cp in state_copies(e, s, d, hin.at[s])])
        each(range(EIGHT), has, lambda d: [cp.wait_send() for cp in state_copies(e, s, d, hin.at[s])])

    def state_fill(e, s):
        img = (imgh, s)
        x = TWO * e + s
        for d in range(TWO):
            put_rows(img, FAR * (1 - d), r_hrow[x, d])
            cst[s, :, pl.ds(272 * (1 - d), SIDE), :] = r_crow[x, d]
            ab = unpack_cols(r_hcol[x, d])
            ec = (1, 0) if d else (FAR, FAR + 1)
            put_col(img, TWO, ec[0], *ab[:TWO])
            put_col(img, TWO, ec[1], *ab[TWO:])
            v = r_ccol[x, d]
            m = MAIN + STRIP * (1 - d) + 1
            cst[s, 0, pl.ds(m, SIDE), :] = v[:SIDE]
            cst[s, 1, pl.ds(m, SIDE), :] = jnp.concatenate(halves(v[SIDE:]), axis=0)
        for d in range(FOUR, EIGHT):
            src = r_diag.at[x, d - FOUR]
            unpack_corner(src, img, d)
            er, ec = corner_dst(d)
            m = MAIN + (STRIP if ec else 0) + (17 if er else 0)
            cst[s, 0, pl.ds(m, 1), :] = src[FOUR:5, :]
            cst[s, 1, pl.ds(m, 1), :] = src[7:EIGHT, :]

    def flag(cond, n):
        return jnp.full((n, L), jnp.where(cond, 1, 0).astype(jnp.int32)) > 0

    def update(s, t, ext, last=False):
        img = (imgh, s)
        z_ref = zext if ext else zpl

        def one(m, n):
            zm = m if ext else m - SIDE
            z = [z_ref[s, p, zm:zm + n, :] for p in range(PIECES)]
            h0, h1, c0, c1 = gates(z, cst[s, 0, m:m + n, :], cst[s, 1, m:m + n, :])
            cst[s, 0, m:m + n, :] = c0
            cst[s, 1, m:m + n, :] = c1
            return h0, h1, c0, c1

        er, end = (1, FAR + 1) if ext else (TWO, FAR)
        while er < end:
            n = 1 if er == 1 or er == end - 1 else TWO
            h0, h1, c0, c1 = one((er - 1) * SIDE, n * SIDE)
            if 1 < er < FAR:
                at = pl.ds(er - TWO, n)
                h_all[t, s, at, :, :L] = h0.reshape(n, SIDE, L)
                h_all[t, s, at, :, L:] = h1[:, :HALF].reshape(n, SIDE, HALF)
            if last:
                c_final[s, at, :, :L] = c0.reshape(n, SIDE, L)
                c_final[s, at, :, L:] = c1[:, :HALF].reshape(n, SIDE, HALF)
            else:
                f0, f1 = h0.astype(F32), h1.astype(F32)
                if er == 1 or er == FAR:
                    ok = flag(has(er // FAR), n * SIDE)
                    f0, f1 = jnp.where(ok, f0, 0.0), jnp.where(ok, f1, 0.0)
                put_body(img, er, f0, f1)
            er += n
        if not ext:
            return
        pos = lax.broadcasted_iota(jnp.int32, (STRIP, L), 0)
        for side in range(TWO):
            ok = flag(has(TWO + side), STRIP) & (flag(has(0), STRIP) | (pos > 0)) & (flag(has(1), STRIP) | (pos < 17))
            h0, h1, _, _ = one(MAIN + STRIP * side, STRIP)
            put_col(img, 1, 1 + 17 * side, jnp.where(ok, h0.astype(F32), 0.0), jnp.where(ok, h1.astype(F32), 0.0))

    def h_build(s, kind):
        build((imgh, s), lhs_h, kind)

    def h_conv(s, kind):
        if kind is PLAIN:
            conv(lhs_h, wh, (gpl, s), (zpl, s), kind, TWO, range(3))
        else:
            conv(lhs_h, wh, (gext, s), (zext, s), kind, 1, range(3))

    load_f[0].wait()
    frame_stage(0)
    load_h.wait()
    load_c.wait()
    def first_state(s, _):
        put_rows((imgh, s), TWO, hin[s])
        v = cin[s].reshape(PLAIN_M, CH)
        at = pl.ds(SIDE, PLAIN_M)
        cst[s, 0, at, :] = v[:, :L]
        cst[s, 1, at, :] = twice(v[:, L:])
        state_stage(s)
        return 0

    lax.fori_loop(0, TWO, first_state, 0)
    near_rows = 1 + has(0).astype(jnp.int32) + has(1).astype(jnp.int32)
    near_cols = 1 + has(TWO).astype(jnp.int32) + has(3).astype(jnp.int32)
    pl.semaphore_wait(barrier, near_rows * near_cols - 1)
    frame_send(0, 0)
    frame_send(0, 1)

    def first_send(s, _):
        state_send(0, s, hin.at[s])
        return 0

    lax.fori_loop(0, TWO, first_send, 0)
    each(range(EIGHT), lambda d: jnp.logical_not(has(OPP[d])), blank)
    load_b.wait()
    for p in range(PIECES):
        bias[p:p + 1, :] = bias_v[pl.ds(p * L, L)].reshape(1, L)
    for cp in load_w[0]:
        cp.wait()
    def first_x(s, _):
        for odd in range(TWO):
            x_build(0, odd, s, IN)
            x_conv(s, odd, IN)
        return 0

    lax.fori_loop(0, TWO, first_x, 0)
    for cp in load_w[1] + load_f[1:]:
        cp.wait()

    def stage_body(k, _):
        frame_stage(k)
        frame_send(k, 0)
        frame_send(k, 1)
        return 0

    lax.fori_loop(1, FOUR, stage_body, 0)
    def first_h(s, _):
        h_build(s, IN)
        h_conv(s, IN)
        return 0

    def first_border(s, _):
        for odd in range(TWO):
            kind = PLAIN_OUT if odd else EXT_OUT
            frame_fill(0, odd, s)
            x_build(0, odd, s, kind)
            x_conv(s, odd, kind)
        return 0

    lax.fori_loop(0, TWO, first_h, 0)
    frame_wait(0)
    lax.fori_loop(0, TWO, first_border, 0)

    def round_body(k, _):
        frame_wait(k + 1)
        for s in range(TWO):
            state_wait(k, s)
            state_fill(k, s)
            h_build(s, EXT_OUT)
            h_conv(s, EXT_OUT)
            frame_fill(k + 1, 0, s)
            x_build(k + 1, 0, s, EXT)
            x_conv(s, 0, EXT, (0, 1))
            update(s, TWO * k, True)
            h_build(s, PLAIN)
            h_conv(s, PLAIN)
            frame_fill(k + 1, 1, s)
            x_build(k + 1, 1, s, PLAIN)
            x_conv(s, 0, EXT, (TWO,))
            x_conv(s, 1, PLAIN, (0,))
            update(s, TWO * k + 1, False)
            state_stage(s)
            state_send(k + 1, s, h_all.at[TWO * k + 1, s])
            h_build(s, IN)
            x_conv(s, 1, PLAIN, (1, TWO))
            h_conv(s, IN)
        return 0

    lax.fori_loop(0, 3, round_body, 0)
    last = 3
    for s in range(TWO):
        state_wait(last, s)
        state_fill(last, s)
        h_build(s, EXT_OUT)
        h_conv(s, EXT_OUT)
        if s == 0:
            update(0, TWO * last, True)
    h_build(0, PLAIN)
    h_conv(0, PLAIN)
    update(1, TWO * last, True)
    h_build(1, PLAIN)
    update(0, TWO * last + 1, False, True)
    h_conv(1, PLAIN)
    update(1, TWO * last + 1, False, True)


def solution(mesh):
    shape = (mesh.shape["rows"], mesh.shape["cols"])
    frame_spec = P(None, "batch", "rows", "cols", None)
    state_spec = P("batch", "rows", "cols", None)
    any_spec = pl.BlockSpec(memory_space=pl.ANY)
    vmem = pl.BlockSpec(memory_space=pltpu.VMEM)

    def local_run(frames, w_x, w_h, gate_bias, h_init, c_init):
        V = pltpu.VMEM
        D = pltpu.SemaphoreType.DMA
        lhs = [V((20, SIDE, TAPS), BF), V((MAIN + STRIP_M, TWO * L), BF), V((3, STRIP_M, TAPS), BF)]
        pair = (TWO, TWO)
        scratch = [
            V(frames.shape, BF), V(h_init.shape, BF), V(c_init.shape, F32), V(gate_bias.shape, F32), V((EIGHT, L), F32),
            V((9 * CH, GATES), BF), V((9 * CH, GATES), BF),
            V((SIDE, TWO, IMG_ROWS, PITCH, L), F32), V(pair + (IMG_ROWS, PITCH, L), F32), V(pair + (EXT_M, L), F32),
            *lhs, *lhs, *lhs,
            V((TWO, PIECES, EXT_M, L), F32), V((TWO, PIECES, PLAIN_M, L), F32), V((TWO, PIECES, EXT_M, L), F32), V((TWO, PIECES, PLAIN_M, L), F32),
            V((EIGHT, TWO, TWO, 3, SIDE, L), BF), V((FOUR, FOUR, TWO, EIGHT, L), F32),
            V((EIGHT, TWO, TWO, TWO, SIDE, CH), BF), V((EIGHT, TWO, TWO, 3, SIDE, L), BF), V((FOUR, FOUR, TWO, EIGHT, L), F32),
            V(pair + (3, SIDE, L), BF), V(pair + (STRIP, L), F32), V((TWO, FOUR, EIGHT, L), F32),
            V((EIGHT, TWO, TWO, SIDE, CH), BF), V((EIGHT, TWO, 3, SIDE, L), BF), V((EIGHT, TWO, TWO, SIDE, L), F32), V((EIGHT, TWO, STRIP, L), F32), V((EIGHT, FOUR, EIGHT, L), F32),
            D((7,)), D((TWO, FAR)), D((EIGHT, EIGHT)), D((EIGHT, EIGHT)), D((EIGHT, 12)), D((EIGHT, 12)),
        ]
        return pl.pallas_call(
            functools.partial(kernel, shape=shape),
            out_shape=[V(frames.shape, BF), V(c_init.shape, F32)],
            in_specs=[any_spec] * 6,
            out_specs=[vmem, vmem],
            scratch_shapes=scratch,
            compiler_params=pltpu.CompilerParams(collective_id=0, has_side_effects=True, vmem_limit_bytes=60 * 1024 * 1024),
            name="convlstm",
        )(frames, w_x, w_h, gate_bias, h_init, c_init)

    return jax.shard_map(local_run, mesh=mesh, in_specs=(frame_spec, P(), P(), P(), state_spec, state_spec), out_specs=(frame_spec, state_spec), check_vma=False)
```

time: 320 us -> 51.1 us (0.16); the launches traced: 315 us -> 51 us
  starting transfers between devices: 111 us -> 0 us
  local copies, waits for them, and re-layouts: 76.3 us -> 2.11 us
  matrix products: 66.9 us -> 0 us
  Pallas kernels: 0 us -> 48.2 us
  other arithmetic: 43.7 us -> 0 us
  waiting for transfers between devices: 15.7 us -> 0 us
    ppermute x36 -> x0, starting transfers between devices: 111 us -> none  [the longest x18 57.9 us: edge_swap(): from_next = lax.ppermute(low_edge, axis_label, up_pairs)]
    dot_general x16 -> x0, matrix products: 66.9 us -> none  [conv_taps(): jnp.dot(flat_patches, flat_weights, preferred_element_type=jnp.float32)]
    pallas_call x0 -> x1, Pallas kernels: none -> 48.2 us  [local_run(): pl.pallas_call(functools.partial(kernel, shape=shape), out_shape=[V(frame...]
    concatenate x25 -> x0, local copies, waits for them, and re-layouts: 40.8 us -> none  [the longest x16 40.8 us: conv_taps(): patches = jnp.concatenate(tap_list, axis=-1)]
    concatenate x17 -> x0, other arithmetic: 31.7 us -> none  [edge_swap(): return jnp.concatenate([from_prev, tile_arr, from_next], axis=split_dim)]
    ppermute x36 -> x0, waiting for transfers between devices: 15.7 us -> none  [the longest x18 8.9 us: edge_swap(): from_prev = lax.ppermute(high_edge, axis_label, down_pairs)]
    while x56 -> x0, local copies, waits for them, and re-layouts: 12.2 us -> none
    dynamic_update_slice x8 -> x0, other arithmetic: 12 us -> none  [local_run(): final_pair, all_hidden = lax.scan(step_fn, (h_init, c_init), frames_ext)]
  transfers between devices with their start and end apart: 36 -> 0, of which waited for: 10 -> 0; matrix products, arithmetic and copies ran while one was open for 24% -> 0% of each run, Pallas kernels for 0% -> 0%
where the time goes in v3:
time: 51.1 us; the launch traced here: 51 us
  Pallas kernels  48.2 us (94%)
  local copies, waits for them, and re-layouts  2.11 us (4%)
  between operations  0.64 us (1%)
    pallas_call x1, Pallas kernels, local_run(): pl.pallas_call(functools.partial(kernel, shape=shape), out_shape=[V(frame...  48.2 us
    unnamed x2, local copies, waits for them, and re-layouts  2.11 us

profile of v3, /device:TPU:97, one launch (start us, length us, event | category | flops | bytes accessed | tf_op | source)
XLA Modules:
  0.0 51.0 jit_solution(5538431867797493408)
XLA Ops:
  0.6 48.2 %convlstm.1 = (bf16[8,2,16,16,192]{4,3,2,1,0:T(8,128)(2,1)S(1)}, f32[2,16,16,192]{3,2,1,0:T(8,128)S(1)}) custom-call(bf16[8,2,16,16,192]{4,3,2,1,0:T(8,128)(2,1)} %frames.1, bf16[3,3,192,768]{3,2,1,0:T(8,128)(2,1)} %w_x.1, bf16[3,3,192,768]{3,2,1,0:T(8,128)(2,1)} %w_h.1, f32[768]{0:T(1024)} %bias_in.1, bf16[2,16,16,192]{3,2,1,0:T(8,128)(2,1)} %h_init.1, ...), custom_call_target="tpu_custom_call" | custom-call | tf_op jit(solution)/shard_map/convlstm/pallas_call | solution.py:588
  48.8 1.3 %copy.10 = bf16[8,2,16,16,192]{4,3,2,1,0:T(8,128)(2,1)} copy(bf16[8,2,16,16,192]{4,3,2,1,0:T(8,128)(2,1)S(1)} %get-tuple-element.2) | data formatting | bytes 3145728
  50.2 0.8 %copy.11 = f32[2,16,16,192]{3,2,1,0:T(8,128)} copy(f32[2,16,16,192]{3,2,1,0:T(8,128)S(1)} %get-tuple-element.3) | data formatting | bytes 786432

commit v4 on v3

--- a/solution.py
+++ b/solution.py
@@ -238,12 +238,12 @@
 
 
 def kernel(frames, w_x, w_h, bias_in, h_init, c_init, h_all, c_final,
-           fr, hin, cin, bias_v, bias, wx, wh, imgx, imgh, cst, tapx, tailx, stripx, tapy, taily, stripy, taph, tailh, striph,
+           fr, hin, cin, bias_v, bias, wx, wh, imgx, imgh, cst, tapx, tailx, stripx, tapy, taily, stripy, taph, tailh, striph, tapi, taili,
            gext, gpl, zext, zpl,
            s_xcol, s_xdiag, r_xrow, r_xcol, r_xdiag,
            s_hcol, s_ccol, s_diag, r_hrow, r_hcol, r_crow, r_ccol, r_diag,
            lsem, wsem, xs_sem, xr_sem, e_s, e_r, *, shape):
-    lhs_x, lhs_y, lhs_h = (tapx, tailx, stripx), (tapy, taily, stripy), (taph, tailh, striph)
+    lhs_x, lhs_y, lhs_h, lhs_i = (tapx, tailx, stripx), (tapy, taily, stripy), (taph, tailh, striph), (tapi, taili, None)
     n_rows, n_cols = shape
     row, col = lax.axis_index("rows"), lax.axis_index("cols")
     grp = lax.axis_index("batch")
@@ -256,11 +256,23 @@
     def peer(d):
         return (grp, col + DIRS[d][1], row + DIRS[d][0])
 
-    def each(dirs, ok, f):
+    have = [has(d) for d in range(EIGHT)]
+
+    def each(f, dirs=(TWO, 3, FOUR, 5, 6, 7, 0, 1)):
         for d in dirs:
-            @pl.when(ok(d))
+            @pl.when(have[d])
             def _(d=d):
                 f(d)
+
+    def start(copies):
+        for cp in copies:
+            cp.start()
+
+    def exchanged(copies, d):
+        for cp in copies(OPP[d]):
+            cp.wait_recv()
+        for cp in copies(d):
+            cp.wait_send()
 
     load_h = pltpu.make_async_copy(h_init, hin, lsem.at[0])
     load_c = pltpu.make_async_copy(c_init, cin, lsem.at[1])
@@ -273,11 +285,10 @@
                 at = dr * TAPS + 3 * L + dc * HALF if dc < TWO else 3 * TAPS + dr * HALF
                 for c_at, n, k_at in ((0, L, dr * TAPS + dc * L), (L, HALF, at)):
                     load_w[i].append(pltpu.make_async_copy(src.at[dr, dc, pl.ds(c_at, n)], dst.at[pl.ds(k_at, n)], wsem.at[i, len(load_w[i])]))
-    for cp in [load_f[0], load_h, load_c, load_b] + load_w[0] + load_w[1] + load_f[1:]:
-        cp.start()
+    start([load_f[0], load_h, load_c, load_b] + load_w[0])
 
     barrier = pltpu.get_barrier_semaphore()
-    each(range(EIGHT), has, lambda d: pl.semaphore_signal(barrier, inc=1, device_id=peer(d), device_id_type=MESH))
+    each(lambda d: pl.semaphore_signal(barrier, inc=1, device_id=peer(d), device_id_type=MESH))
 
     def blank(d):
         refs = (r_xrow, r_hrow, r_crow) if d < TWO else (r_xcol, r_hcol, r_ccol) if d < FOUR else (r_xdiag, r_diag)
@@ -313,12 +324,11 @@
             return mk(s_xcol.at[f, d - TWO, pl.ds(0, n)], r_xcol.at[f, d - TWO, pl.ds(0, n)])
         return [] if odd else mk(s_xdiag.at[k, d - FOUR], r_xdiag.at[k, d - FOUR])
 
-    def frame_send(k, odd):
-        each(range(FOUR) if odd else (TWO, 3, FOUR, 5, 6, 7, 0, 1), has, lambda d: [cp.start() for cp in frame_copies(k, odd, d)])
+    def both_frames(k):
+        return lambda d: frame_copies(k, 0, d) + frame_copies(k, 1, d)
 
     def frame_wait(k):
-        each(range(EIGHT), lambda d: has(OPP[d]), lambda d: [cp.wait_recv() for odd in range(TWO) for cp in frame_copies(k, odd, d)])
-        each(range(EIGHT), has, lambda d: [cp.wait_send() for odd in range(TWO) for cp in frame_copies(k, odd, d)])
+        each(lambda d: exchanged(both_frames(k), d))
 
     def frame_fill(k, odd, s):
         f = TWO * k + odd
@@ -350,7 +360,7 @@
     def x_conv(s, odd, kind, parts=range(3)):
         conv(lhs_y if odd else lhs_x, wx, bias, (gpl if odd else gext, s), kind, 1 + odd, parts)
 
-    def state_copies(e, s, d, hsrc, which=(0, 1)):
+    def state_copies(e, s, d, hsrc):
         x = TWO * e + s
         if d < TWO:
             refs = ((hsrc.at[pl.ds(INNER * d, TWO)], r_hrow.at[x, d]), (cst.at[s, :, pl.ds(SIDE + 240 * d, SIDE)], r_crow.at[x, d]))
@@ -358,7 +368,7 @@
             refs = ((s_hcol.at[s, d - TWO], r_hcol.at[x, d - TWO]), (s_ccol.at[s, d - TWO], r_ccol.at[x, d - TWO]))
         else:
             refs = ((s_diag.at[s, d - FOUR], r_diag.at[x, d - FOUR]),)
-        return [pltpu.make_async_remote_copy(src_ref=refs[i][0], dst_ref=refs[i][1], send_sem=e_s.at[x, d + EIGHT * i], recv_sem=e_r.at[x, d + EIGHT * i], device_id=peer(d), device_id_type=MESH) for i in which[:len(refs)]]
+        return [pltpu.make_async_remote_copy(src_ref=refs[i][0], dst_ref=refs[i][1], send_sem=e_s.at[x, d + EIGHT * i], recv_sem=e_r.at[x, d + EIGHT * i], device_id=peer(d), device_id_type=MESH) for i in range(len(refs))]
 
     def state_stage(s):
         img = (imgh, s)
@@ -374,12 +384,10 @@
             pack_corner(s_diag.at[s, d - FOUR], img, d, cst[s, 0, at, :], cst[s, 1, at, :])
 
     def state_send(e, s, hsrc):
-        each((TWO, 3, FOUR, 5, 6, 7, 0, 1), has, lambda d: state_copies(e, s, d, hsrc, (0,))[0].start())
-        each(range(FOUR), has, lambda d: state_copies(e, s, d, hsrc, (1,))[0].start())
+        each(lambda d: start(state_copies(e, s, d, hsrc)))
 
     def state_wait(e, s):
-        each(range(EIGHT), lambda d: has(OPP[d]), lambda d: [cp.wait_recv() for cp in state_copies(e, s, d, hin.at[s])])
-        each(range(EIGHT), has, lambda d: [cp.wait_send() for cp in state_copies(e, s, d, hin.at[s])])
+        each(lambda d: exchanged(lambda d: state_copies(e, s, d, hin.at[s]), d))
 
     def state_fill(e, s):
         img = (imgh, s)
@@ -403,6 +411,9 @@
             cst[s, 0, pl.ds(m, 1), :] = src[FOUR:5, :]
             cst[s, 1, pl.ds(m, 1), :] = src[7:EIGHT, :]
 
+    def at_side(d):
+        return have[d]
+
     def flag(cond, n):
         return jnp.full((n, L), jnp.where(cond, 1, 0).astype(jnp.int32)) > 0
 
@@ -432,7 +443,7 @@
             else:
                 f0, f1 = h0.astype(F32), h1.astype(F32)
                 if er == 1 or er == FAR:
-                    ok = flag(has(er // FAR), n * SIDE)
+                    ok = flag(at_side(er // FAR), n * SIDE)
                     f0, f1 = jnp.where(ok, f0, 0.0), jnp.where(ok, f1, 0.0)
                 put_body(img, er, f0, f1)
             er += n
@@ -440,18 +451,18 @@
             return
         pos = lax.broadcasted_iota(jnp.int32, (STRIP, L), 0)
         for side in range(TWO):
-            ok = flag(has(TWO + side), STRIP) & (flag(has(0), STRIP) | (pos > 0)) & (flag(has(1), STRIP) | (pos < 17))
+            ok = flag(at_side(TWO + side), STRIP) & (flag(at_side(0), STRIP) | (pos > 0)) & (flag(at_side(1), STRIP) | (pos < 17))
             h0, h1, _, _ = one(MAIN + STRIP * side, STRIP)
             put_col(img, 1, 1 + 17 * side, jnp.where(ok, h0.astype(F32), 0.0), jnp.where(ok, h1.astype(F32), 0.0))
 
     def h_build(s, kind):
-        build((imgh, s), lhs_h, kind)
+        build((imgh, s), lhs_i if kind is IN else lhs_h, kind)
 
     def h_conv(s, kind):
         if kind is PLAIN:
             conv(lhs_h, wh, (gpl, s), (zpl, s), kind, TWO, range(3))
         else:
-            conv(lhs_h, wh, (gext, s), (zext, s), kind, 1, range(3))
+            conv(lhs_i if kind is IN else lhs_h, wh, (gext, s), (zext, s), kind, 1, range(3))
 
     load_f[0].wait()
     frame_stage(0)
@@ -467,61 +478,53 @@
         return 0
 
     lax.fori_loop(0, TWO, first_state, 0)
-    near_rows = 1 + has(0).astype(jnp.int32) + has(1).astype(jnp.int32)
-    near_cols = 1 + has(TWO).astype(jnp.int32) + has(3).astype(jnp.int32)
+    near_rows = 1 + have[0].astype(jnp.int32) + have[1].astype(jnp.int32)
+    near_cols = 1 + have[TWO].astype(jnp.int32) + have[3].astype(jnp.int32)
     pl.semaphore_wait(barrier, near_rows * near_cols - 1)
-    frame_send(0, 0)
-    frame_send(0, 1)
-
-    def first_send(s, _):
-        state_send(0, s, hin.at[s])
-        return 0
-
-    lax.fori_loop(0, TWO, first_send, 0)
-    each(range(EIGHT), lambda d: jnp.logical_not(has(OPP[d])), blank)
+    each(lambda d: start(frame_copies(0, 0, d) + state_copies(0, 0, d, hin.at[0]) + frame_copies(0, 1, d) + state_copies(0, 1, d, hin.at[1])))
+    start(load_w[1] + load_f[1:])
+    for d in range(EIGHT):
+        @pl.when(jnp.logical_not(have[OPP[d]]))
+        def _(d=d):
+            blank(d)
     load_b.wait()
     for p in range(PIECES):
         bias[p:p + 1, :] = bias_v[pl.ds(p * L, L)].reshape(1, L)
     for cp in load_w[0]:
         cp.wait()
-    def first_x(s, _):
-        for odd in range(TWO):
+    for s in range(TWO):
+        for odd in range(TWO - s):
             x_build(0, odd, s, IN)
             x_conv(s, odd, IN)
-        return 0
-
-    lax.fori_loop(0, TWO, first_x, 0)
     for cp in load_w[1] + load_f[1:]:
         cp.wait()
 
     def stage_body(k, _):
         frame_stage(k)
-        frame_send(k, 0)
-        frame_send(k, 1)
+        each(lambda d: start(both_frames(k)(d)))
         return 0
 
     lax.fori_loop(1, FOUR, stage_body, 0)
-    def first_h(s, _):
+    h_build(0, IN)
+    h_conv(0, IN)
+    frame_wait(0)
+    for s in range(TWO):
+        for odd in range(TWO):
+            kind = (PLAIN if s else PLAIN_OUT) if odd else EXT_OUT
+            frame_fill(0, odd, s)
+            x_build(0, odd, s, kind)
+            x_conv(s, odd, kind, (0,) if kind is PLAIN else range(3))
+
+    def left_over(s):
+        x_conv(s, 1, PLAIN, (1, TWO))
         h_build(s, IN)
         h_conv(s, IN)
-        return 0
-
-    def first_border(s, _):
-        for odd in range(TWO):
-            kind = PLAIN_OUT if odd else EXT_OUT
-            frame_fill(0, odd, s)
-            x_build(0, odd, s, kind)
-            x_conv(s, odd, kind)
-        return 0
-
-    lax.fori_loop(0, TWO, first_h, 0)
-    frame_wait(0)
-    lax.fori_loop(0, TWO, first_border, 0)
 
     def round_body(k, _):
         frame_wait(k + 1)
         for s in range(TWO):
             state_wait(k, s)
+            left_over(1 - s)
             state_fill(k, s)
             h_build(s, EXT_OUT)
             h_conv(s, EXT_OUT)
@@ -538,15 +541,14 @@
             update(s, TWO * k + 1, False)
             state_stage(s)
             state_send(k + 1, s, h_all.at[TWO * k + 1, s])
-            h_build(s, IN)
-            x_conv(s, 1, PLAIN, (1, TWO))
-            h_conv(s, IN)
         return 0
 
     lax.fori_loop(0, 3, round_body, 0)
     last = 3
     for s in range(TWO):
         state_wait(last, s)
+        if s == 0:
+            left_over(1)
         state_fill(last, s)
         h_build(s, EXT_OUT)
         h_conv(s, EXT_OUT)
@@ -577,7 +579,7 @@
             V(frames.shape, BF), V(h_init.shape, BF), V(c_init.shape, F32), V(gate_bias.shape, F32), V((EIGHT, L), F32),
             V((9 * CH, GATES), BF), V((9 * CH, GATES), BF),
             V((SIDE, TWO, IMG_ROWS, PITCH, L), F32), V(pair + (IMG_ROWS, PITCH, L), F32), V(pair + (EXT_M, L), F32),
-            *lhs, *lhs, *lhs,
+            *lhs, *lhs, *lhs, *lhs[:TWO],
             V((TWO, PIECES, EXT_M, L), F32), V((TWO, PIECES, PLAIN_M, L), F32), V((TWO, PIECES, EXT_M, L), F32), V((TWO, PIECES, PLAIN_M, L), F32),
             V((EIGHT, TWO, TWO, 3, SIDE, L), BF), V((FOUR, FOUR, TWO, EIGHT, L), F32),
             V((EIGHT, TWO, TWO, TWO, SIDE, CH), BF), V((EIGHT, TWO, TWO, 3, SIDE, L), BF), V((FOUR, FOUR, TWO, EIGHT, L), F32),

time: 51.1 us -> 50.1 us (0.980)
  Pallas kernels: 48.2 us -> 47.2 us
    pallas_call x1, Pallas kernels: 48.2 us -> 47.2 us  [local_run(): pl.pallas_call(functools.partial(kernel, shape=shape), out_shape=[V(frame...]
where the time goes in v4:
time: 50.1 us; the launch traced here: 49.9 us
  Pallas kernels  47.2 us (94%)
  local copies, waits for them, and re-layouts  2.11 us (4%)
  between operations  0.64 us (1%)
    pallas_call x1, Pallas kernels, local_run(): pl.pallas_call(functools.partial(kernel, shape=shape), out_shape=[V(frame...  47.2 us
    unnamed x2, local copies, waits for them, and re-layouts  2.11 us

profile of v4, /device:TPU:97, one launch (start us, length us, event | category | flops | bytes accessed | tf_op | source)
XLA Modules:
  0.0 49.9 jit_solution(14599904302393021150)
XLA Ops:
  0.6 47.2 %convlstm.1 = (bf16[8,2,16,16,192]{4,3,2,1,0:T(8,128)(2,1)S(1)}, f32[2,16,16,192]{3,2,1,0:T(8,128)S(1)}) custom-call(bf16[8,2,16,16,192]{4,3,2,1,0:T(8,128)(2,1)} %frames.1, bf16[3,3,192,768]{3,2,1,0:T(8,128)(2,1)} %w_x.1, bf16[3,3,192,768]{3,2,1,0:T(8,128)(2,1)} %w_h.1, f32[768]{0:T(1024)} %bias_in.1, bf16[2,16,16,192]{3,2,1,0:T(8,128)(2,1)} %h_init.1, ...), custom_call_target="tpu_custom_call" | custom-call | tf_op jit(solution)/shard_map/convlstm/pallas_call | solution.py:590
  47.8 1.3 %copy.10 = bf16[8,2,16,16,192]{4,3,2,1,0:T(8,128)(2,1)} copy(bf16[8,2,16,16,192]{4,3,2,1,0:T(8,128)(2,1)S(1)} %get-tuple-element.2) | data formatting | bytes 3145728
  49.2 0.8 %copy.11 = f32[2,16,16,192]{3,2,1,0:T(8,128)} copy(f32[2,16,16,192]{3,2,1,0:T(8,128)S(1)} %get-tuple-element.3) | data formatting | bytes 786432

commit v5 on v4

--- a/solution.py
+++ b/solution.py
@@ -552,8 +552,7 @@
         state_fill(last, s)
         h_build(s, EXT_OUT)
         h_conv(s, EXT_OUT)
-        if s == 0:
-            update(0, TWO * last, True)
+    update(0, TWO * last, True)
     h_build(0, PLAIN)
     h_conv(0, PLAIN)
     update(1, TWO * last, True)

time: 50.1 us -> 50.2 us (level)
  no operation moved by 1% of the time
where the time goes in v5:
time: 50.2 us; the launch traced here: 50.1 us
  Pallas kernels  47.3 us (94%)
  local copies, waits for them, and re-layouts  2.11 us (4%)
  between operations  0.64 us (1%)
    pallas_call x1, Pallas kernels, local_run(): pl.pallas_call(functools.partial(kernel, shape=shape), out_shape=[V(frame...  47.3 us
    unnamed x2, local copies, waits for them, and re-layouts  2.11 us

profile of v5, /device:TPU:97, one launch (start us, length us, event | category | flops | bytes accessed | tf_op | source)
XLA Modules:
  0.0 50.1 jit_solution(17849767229680750470)
XLA Ops:
  0.6 47.3 %convlstm.1 = (bf16[8,2,16,16,192]{4,3,2,1,0:T(8,128)(2,1)S(1)}, f32[2,16,16,192]{3,2,1,0:T(8,128)S(1)}) custom-call(bf16[8,2,16,16,192]{4,3,2,1,0:T(8,128)(2,1)} %frames.1, bf16[3,3,192,768]{3,2,1,0:T(8,128)(2,1)} %w_x.1, bf16[3,3,192,768]{3,2,1,0:T(8,128)(2,1)} %w_h.1, f32[768]{0:T(1024)} %bias_in.1, bf16[2,16,16,192]{3,2,1,0:T(8,128)(2,1)} %h_init.1, ...), custom_call_target="tpu_custom_call" | custom-call | tf_op jit(solution)/shard_map/convlstm/pallas_call | solution.py:589
  48.0 1.3 %copy.10 = bf16[8,2,16,16,192]{4,3,2,1,0:T(8,128)(2,1)} copy(bf16[8,2,16,16,192]{4,3,2,1,0:T(8,128)(2,1)S(1)} %get-tuple-element.2) | data formatting | bytes 3145728
  49.3 0.8 %copy.11 = f32[2,16,16,192]{3,2,1,0:T(8,128)} copy(f32[2,16,16,192]{3,2,1,0:T(8,128)S(1)} %get-tuple-element.3) | data formatting | bytes 786432
